TPU v7x, 32 devices: a whole 2x2x4 slice. The times are simulated.
32 devices in a mesh: rep: 4 (over z), exp: 8 (over y, x, core).
Axes of the slice: x: 2, y: 2, z: 4, core: 2. Of those that a mesh axis runs over, the one named last changes fastest.
Arguments:
- tokens: bfloat16 [64, 128, 512], P('rep', 'exp'), may hold values from -48 to 48
- gate: float32 [64, 128], P('rep', 'exp'), may hold values from 0.25 to 1
- route: int32 [4, 8, 256, 1], P('rep', 'exp'), may hold values from 0 to 7; in each aligned block of 256 rows (0 to 255, 256 to 511, ..., all dimensions but the last counted through in order) at most 48 rows name the same one
- cotangent: bfloat16 [64, 128, 512], P('rep', 'exp'), may hold values from -6 to 6
- w_qkv: bfloat16 [512, 1536], replicated, may hold values from -1 to 1
- w_proj: bfloat16 [512, 512], replicated, may hold values from -0.25 to 0.25
- w_up: bfloat16 [8, 2048, 512], P('exp', 'rep'), may hold values from -0.25 to 0.25
- w_down: bfloat16 [8, 2048, 512], P('exp', 'rep'), may hold values from -0.125 to 0.125
Outputs:
- layer_out: bfloat16 [64, 128, 512], P('rep', 'exp')
- input_grad: bfloat16 [64, 128, 512], P('rep', 'exp')
- grad_up: float32 [8, 2048, 512], P('exp', 'rep')
- grad_down: float32 [8, 2048, 512], P('exp', 'rep')
Inputs may be any that keep to these rules, and one draw needn't show every extreme that they name: `route`: among the tokens of one tile no expert is named more than 48 times.
All inputs are finite; a program needn't handle non-finite values.
Results may differ from a plain program's by a relative error of at most 0.018.
Values may be sent and summed in bfloat16 or wider, within the bound.
A program may use at most 64 MiB of HBM per device.

v0:
```python
import math

import jax
import jax.numpy as jnp
from jax import lax
from jax.sharding import PartitionSpec as P

HEADS = 16


GELU_C = math.sqrt(2.0 / math.pi)
window_side = 8
margin_cells = 4


def padded(block, sides, width):
    for axis, dim in sides:
        count = lax.axis_size(axis)
        forward = [(i, i + 1) for i in range(count - 1)]
        backward = [(target, source) for source, target in forward]
        low = lax.ppermute(
            lax.slice_in_dim(block, block.shape[dim] - width, None, axis=dim), axis, forward
        )
        high = lax.ppermute(lax.slice_in_dim(block, 0, width, axis=dim), axis, backward)
        block = jnp.concatenate([low, block, high], axis=dim)
    return block


def gelu_tanh(inputs):
    return 0.5 * inputs * (1.0 + jnp.tanh(GELU_C * (inputs + 0.044715 * inputs * inputs * inputs)))


def gelu_slope(inputs):
    inner = jnp.tanh(GELU_C * (inputs + 0.044715 * inputs * inputs * inputs))
    return 0.5 * (1.0 + inner) + 0.5 * inputs * (1.0 - inner * inner) * GELU_C * (
        1.0 + 3.0 * 0.044715 * inputs * inputs
    )


def layer_norm(values):
    average = jnp.mean(values, axis=-1, keepdims=True)
    centred = values - average
    spread = jnp.mean(centred * centred, axis=-1, keepdims=True)
    return centred * lax.rsqrt(spread + 1e-05)


def window_attend(qkv, in_grid):
    ext_rows, ext_cols, triple = qkv.shape
    feature = triple // 3
    head_size = feature // HEADS
    win_rows = ext_rows // window_side
    win_cols = ext_cols // window_side
    cells = window_side * window_side
    blocks = qkv.reshape(win_rows, window_side, win_cols, window_side, triple).transpose(
        0, 2, 1, 3, 4
    )
    blocks = blocks.reshape(win_rows * win_cols, cells, 3, HEADS, head_size)
    present = (
        in_grid.reshape(win_rows, window_side, win_cols, window_side)
        .transpose(0, 2, 1, 3)
        .reshape(win_rows * win_cols, cells)
    )
    scores = jnp.einsum(
        "wqhd,wkhd->whqk", blocks[:, :, 0], blocks[:, :, 1], preferred_element_type=jnp.float32
    ) / math.sqrt(head_size)
    scores = jnp.where(present[:, None, None, :], scores, jnp.float32(-1e30))
    peak_score = jnp.max(scores, axis=-1, keepdims=True)
    weights = jnp.exp(scores - peak_score)
    probabilities = (weights / jnp.sum(weights, axis=-1, keepdims=True)).astype(jnp.bfloat16)
    context = jnp.einsum(
        "whqk,wkhd->wqhd", probabilities, blocks[:, :, 2], preferred_element_type=jnp.float32
    ).astype(jnp.bfloat16)
    context = context.reshape(win_rows, win_cols, window_side, window_side, feature).transpose(
        0, 2, 1, 3, 4
    )
    return context.reshape(ext_rows, ext_cols, feature)


def per_device(tokens, gate, route, cotangent, w_qkv, w_proj, w_up, w_down):
    tile_rows, tile_cols, feature = tokens.shape
    tok_count = tile_rows * tile_cols
    ext_rows = tile_rows + 2 * margin_cells
    ext_cols = tile_cols + 2 * margin_cells
    extended = padded(tokens, (("rep", 0), ("exp", 1)), 4)
    qkv = jnp.dot(extended.reshape(-1, feature), w_qkv, preferred_element_type=jnp.float32).astype(
        jnp.bfloat16
    )
    qkv = qkv.reshape(ext_rows, ext_cols, 3 * feature)
    row_ids = (
        lax.axis_index("rep") * tile_rows - margin_cells + jnp.arange(ext_rows, dtype=jnp.int32)
    )
    col_ids = (
        lax.axis_index("exp") * tile_cols - margin_cells + jnp.arange(ext_cols, dtype=jnp.int32)
    )
    row_inside = (row_ids >= 0) & (row_ids < tile_rows * lax.axis_size("rep"))
    col_inside = (col_ids >= 0) & (col_ids < tile_cols * lax.axis_size("exp"))
    in_grid = row_inside[:, None] & col_inside[None, :]
    context = window_attend(qkv, in_grid)[
        margin_cells : tile_rows + margin_cells, margin_cells : tile_cols + margin_cells
    ].reshape(tok_count, feature)
    attended = jnp.dot(context, w_proj, preferred_element_type=jnp.float32)
    flat_tokens = tokens.reshape(tok_count, feature)
    mixed = (flat_tokens.astype(jnp.float32) + layer_norm(attended)).astype(jnp.bfloat16)
    experts = lax.axis_size("exp")
    capacity = max(2, 3 * tok_count // (2 * experts))
    chosen = route.reshape(tok_count)
    matches = (chosen[:, None] == jnp.arange(experts, dtype=jnp.int32)[None, :]).astype(jnp.int32)
    position = jnp.sum(matches * (jnp.cumsum(matches, axis=0) - 1), axis=1)
    target = chosen * capacity + position
    placer = (target[:, None] == jnp.arange(experts * capacity, dtype=jnp.int32)[None, :]).astype(
        jnp.bfloat16
    )
    gate_rows = gate.reshape(tok_count)
    upstream = (
        gate_rows[:, None] * cotangent.reshape(tok_count, feature).astype(jnp.float32)
    ).astype(jnp.bfloat16)

    def to_slots(values):
        placed = lax.dot_general(
            placer, values, (((0,), (0,)), ((), ())), preferred_element_type=jnp.float32
        )
        return placed.astype(jnp.bfloat16).reshape(experts, capacity, feature)

    def from_slots(slot_values):
        return jnp.dot(
            placer,
            slot_values.reshape(experts * capacity, feature),
            preferred_element_type=jnp.float32,
        )

    up_whole, down_whole = (
        lax.all_gather(w_up, "rep", axis=1, tiled=True),
        lax.all_gather(w_down, "rep", axis=1, tiled=True),
    )
    up_mat = up_whole[0]
    down_mat = down_whole[0]

    def forward(sent_x):
        slot_rows = sent_x.reshape(-1, feature)
        pre_act = lax.dot_general(
            slot_rows, up_mat, (((1,), (1,)), ((), ())), preferred_element_type=jnp.float32
        )
        hidden = gelu_tanh(pre_act).astype(jnp.bfloat16)
        expert_out = jnp.dot(hidden, down_mat, preferred_element_type=jnp.float32).astype(
            jnp.bfloat16
        )
        return (slot_rows, pre_act, hidden, expert_out.reshape(-1, capacity, feature))

    def backward(pre_act, sent_g):
        slot_grads = sent_g.reshape(-1, feature)
        hidden_grad = lax.dot_general(
            slot_grads, down_mat, (((1,), (1,)), ((), ())), preferred_element_type=jnp.float32
        )
        pre_grad = (hidden_grad * gelu_slope(pre_act)).astype(jnp.bfloat16)
        input_slots = jnp.dot(pre_grad, up_mat, preferred_element_type=jnp.float32).astype(
            jnp.bfloat16
        )
        return (slot_grads, pre_grad, input_slots.reshape(-1, capacity, feature))

    sent_x = lax.all_to_all(to_slots(mixed), "exp", split_axis=0, concat_axis=0, tiled=True)
    slot_rows, pre_act, hidden, expert_out = forward(sent_x)
    back_out = lax.all_to_all(expert_out, "exp", split_axis=0, concat_axis=0, tiled=True)
    sent_g = lax.all_to_all(to_slots(upstream), "exp", split_axis=0, concat_axis=0, tiled=True)
    slot_grads, pre_grad, input_slots = backward(pre_act, sent_g)
    back_grad = lax.all_to_all(input_slots, "exp", split_axis=0, concat_axis=0, tiled=True)
    layer_out = (mixed.astype(jnp.float32) + gate_rows[:, None] * from_slots(back_out)).astype(
        jnp.bfloat16
    )
    input_grad = from_slots(back_grad).astype(jnp.bfloat16)
    up_part = lax.dot_general(
        pre_grad, slot_rows, (((0,), (0,)), ((), ())), preferred_element_type=jnp.float32
    )
    down_part = lax.dot_general(
        hidden, slot_grads, (((0,), (0,)), ((), ())), preferred_element_type=jnp.float32
    )
    summed = lax.psum_scatter(
        jnp.concatenate([up_part, down_part], axis=1).astype(jnp.bfloat16),
        "rep",
        scatter_dimension=0,
        tiled=True,
    ).astype(jnp.float32)
    grad_up_rows = summed[:, :feature]
    grad_down_rows = summed[:, feature:]
    average_factor = 1.0 / lax.axis_size("rep")
    return (
        layer_out.reshape(tile_rows, tile_cols, feature),
        input_grad.reshape(tile_rows, tile_cols, feature),
        (grad_up_rows * average_factor)[None],
        (grad_down_rows * average_factor)[None],
    )


def solution(mesh):
    placed = (
        P("rep", "exp", None),
        P("rep", "exp"),
        P("rep", "exp", None, None),
        P("rep", "exp", None),
        P(),
        P(),
        P("exp", "rep", None),
        P("exp", "rep", None),
    )
    return jax.shard_map(
        per_device,
        mesh=mesh,
        in_specs=placed,
        out_specs=(
            P("rep", "exp", None),
            P("rep", "exp", None),
            P("exp", "rep", None),
            P("exp", "rep", None),
        ),
        check_vma=False,
    )
```

profile of v0, /device:TPU:11, one launch (start us, length us, event | category | flops | bytes accessed | tf_op | source)
XLA Modules:
  0.0 200.2 jit_solution(18126959149087675688)
XLA Ops:
  8.8 3.2 %collective-permute-start = (bf16[4,16,512]{2,1,0:T(8,128)(2,1)S(1)}, bf16[4,16,512]{2,1,0:T(8,128)(2,1)S(1)}, u32[]{:S(2)}, u32[]{:S(2)}) collective-permute-start(bf16[4,16,512]{2,1,0:T(8,128)(2,1)S(1)} %get-tuple-element.20), channel_id=1, source_target_pairs={{0,8},{8,16},{16,24},{1,9},{9,17},{17,25},{2,10},{10,18},{18,26},{... | collective-permute-start | bytes 196616 | tf_op jit(solution)/shard_map/ppermute | solution.py:21
  17.7 3.5 %collective-permute-start.3 = (bf16[24,4,512]{2,1,0:T(4,128)(2,1)S(1)}, bf16[24,4,512]{2,1,0:T(4,128)(2,1)S(1)}, u32[]{:S(2)}, u32[]{:S(2)}) collective-permute-start(bf16[24,4,512]{2,1,0:T(4,128)(2,1)S(1)} %get-tuple-element.18), channel_id=1, source_target_pairs={{1,0},{2,1},{3,2},{4,3},{5,4},{6,5},{7,6},{9,8},{10,9},{11,10},{12... | collective-permute-start | bytes 294920 | tf_op jit(solution)/shard_map/ppermute | solution.py:24
  21.2 3.0 %collective-permute-start.2 = (bf16[24,4,512]{2,1,0:T(4,128)(2,1)S(1)}, bf16[24,4,512]{2,1,0:T(4,128)(2,1)S(1)}, u32[]{:S(2)}, u32[]{:S(2)}) collective-permute-start(bf16[24,4,512]{2,1,0:T(4,128)(2,1)S(1)} %get-tuple-element.17), channel_id=1, source_target_pairs={{0,1},{1,2},{2,3},{3,4},{4,5},{5,6},{6,7},{8,9},{9,10},{10,11},{11... | collective-permute-start | bytes 294920 | tf_op jit(solution)/shard_map/ppermute | solution.py:21
  27.4 6.6 %reshape.134 = bf16[9,64,3,16,32]{4,3,2,1,0:T(8,128)(2,1)} reshape(bf16[3,3,8,8,1536]{4,3,2,1,0:T(8,128)(2,1)S(1)} %bitcast.79) | data formatting | bytes 3538944 | tf_op jit(solution)/shard_map/reshape | solution.py:57
  34.0 6.9 %fusion.56 = (bf16[9,64,1,16,32]{4,3,2,1,0:T(8,128)(2,1)}, bf16[9,64,1,16,32]{4,3,2,1,0:T(8,128)(2,1)}, bf16[9,64,1,16,32]{4,3,2,1,0:T(8,128)(2,1)}) fusion(bf16[9,64,3,16,32]{4,3,2,1,0:T(8,128)(2,1)} %reshape.134), kind=kLoop, calls=%fused_computation.85 | loop fusion | bytes 3538944 | tf_op jit(solution)/shard_map/slice | solution.py:71
  40.9 3.5 %copy.27 = bf16[9,64,1,16,32]{1,4,3,0,2:T(8,128)(2,1)S(1)} copy(bf16[9,64,1,16,32]{4,3,2,1,0:T(8,128)(2,1)} %get-tuple-element.14) | data formatting | bytes 1179648
  44.4 3.5 %copy.26 = bf16[9,64,1,16,32]{1,4,3,0,2:T(8,128)(2,1)S(1)} copy(bf16[9,64,1,16,32]{4,3,2,1,0:T(8,128)(2,1)} %get-tuple-element.13) | data formatting | bytes 1179648
  47.9 4.4 %copy.25 = bf16[9,64,1,16,32]{1,4,3,0,2:T(8,128)(2,1)} copy(bf16[9,64,1,16,32]{4,3,2,1,0:T(8,128)(2,1)} %get-tuple-element.12) | data formatting | bytes 1179648
  56.5 2.9 %copy.20 = bf16[9,64,16,32]{3,2,1,0:T(8,128)(2,1)} copy(bf16[9,64,16,32]{1,3,2,0:T(8,128)(2,1)S(1)} %fusion.21) | data formatting | bytes 1179648 | tf_op jit(solution)/shard_map/convert_element_type | solution.py:72
  59.4 3.8 %reshape.135 = bf16[3,3,8,8,512]{4,3,2,1,0:T(8,128)(2,1)S(1)} reshape(bf16[9,64,16,32]{3,2,1,0:T(8,128)(2,1)} %copy.20) | data formatting | bytes 1179648 | tf_op jit(solution)/shard_map/reshape | solution.py:73
  65.3 5.2 %all-to-all-start = ((bf16[8,48,512]{2,1,0:T(8,128)(2,1)}), bf16[8,48,512]{2,1,0:T(8,128)(2,1)S(1)}, u32[]{:S(2)}, u32[]{:S(2)}) async-start(bf16[8,48,512]{2,1,0:T(8,128)(2,1)} %bitcast.15), calls=%async_computation | async-start | bytes 786432 | tf_op jit(solution)/shard_map/all_to_all | solution.py:160
  71.8 5.6 %all-to-all-done = bf16[8,48,512]{2,1,0:T(8,128)(2,1)S(1)} async-done(((bf16[8,48,512]{2,1,0:T(8,128)(2,1)}), bf16[8,48,512]{2,1,0:T(8,128)(2,1)S(1)}, u32[]{:S(2)}, u32[]{:S(2)}) %all-to-all-start) | async-done | bytes 393248 | tf_op jit(solution)/shard_map/all_to_all | solution.py:160
  77.4 4.8 %all-to-all-start.2 = ((bf16[8,48,512]{2,1,0:T(8,128)(2,1)}), bf16[8,48,512]{2,1,0:T(8,128)(2,1)S(1)}, u32[]{:S(2)}, u32[]{:S(2)}) async-start(bf16[8,48,512]{2,1,0:T(8,128)(2,1)} %bitcast.23), calls=%async_computation.2 | async-start | bytes 786432 | tf_op jit(solution)/shard_map/all_to_all | solution.py:163
  82.2 4.3 %fusion.18 = f32[384,2048]{1,0:T(8,128)} fusion(bf16[384,512]{1,0:T(8,128)(2,1)S(1)} %bitcast.83, bf16[1,2048,512]{2,1,0:T(8,128)(2,1)} %all-gather.3.cloned.1.call-done), kind=kOutput, calls=%fused_computation.28 | convolution fusion | flops 805306368 | bytes 5636096 | tf_op jit(solution)/shard_map/dot_general | solution.py:140
  86.5 2.6 %all-to-all-done.2 = bf16[8,48,512]{2,1,0:T(8,128)(2,1)S(1)} async-done(((bf16[8,48,512]{2,1,0:T(8,128)(2,1)}), bf16[8,48,512]{2,1,0:T(8,128)(2,1)S(1)}, u32[]{:S(2)}, u32[]{:S(2)}) %all-to-all-start.2) | async-done | bytes 393248 | tf_op jit(solution)/shard_map/all_to_all | solution.py:163
  89.1 4.8 %convolution_convert_fusion.1 = bf16[2048,512]{0,1:T(8,128)(2,1)} fusion(bf16[384,512]{1,0:T(8,128)(2,1)S(1)} %bitcast.88, f32[384,2048]{1,0:T(8,128)} %fusion.18), kind=kOutput, calls=%fused_computation.17 | convolution fusion | flops 813432832 | bytes 5636096 | tf_op jit(solution)/shard_map/dot_general | solution.py:173
  94.0 6.7 %all-gather.5.cloned.1.call-done = bf16[1,2048,512]{2,1,0:T(8,128)(2,1)} async-done(((bf16[1,512,512]{2,1,0:T(8,128)(2,1)}), bf16[1,2048,512]{2,1,0:T(8,128)(2,1)}) %all-gather.5.cloned.1.call-update) | async-done | bytes 2097168 | tf_op jit(solution)/shard_map/all_gather | solution.py:133
  100.6 4.7 %fusion.8 = bf16[384,2048]{1,0:T(8,128)(2,1)S(1)} fusion(f32[384,2048]{1,0:T(8,128)} %fusion.18, bf16[384,512]{1,0:T(8,128)(2,1)S(1)} %bitcast.89, bf16[1,2048,512]{2,1,0:T(8,128)(2,1)} %all-gather.5.cloned.1.call-done), kind=kOutput, calls=%fused_computation.14 | convolution fusion | flops 820248576 | bytes 7208960 | tf_op jit(solution)/shard_map/dot_general | solution.py:151
  109.5 3.3 %fusion.22 = bf16[384,512]{1,0:T(8,128)(2,1)} fusion(bf16[384,2048]{1,0:T(8,128)(2,1)S(1)} %fusion.8, bf16[1,2048,512]{2,1,0:T(8,128)(2,1)} %all-gather.3.cloned.1.call-done), kind=kOutput, calls=%fused_computation.33 | convolution fusion | flops 805502976 | bytes 4063232 | tf_op jit(solution)/shard_map/dot_general | solution.py:155
  112.8 5.0 %all-to-all-start.3 = ((bf16[8,48,512]{2,1,0:T(8,128)(2,1)}), bf16[8,48,512]{2,1,0:T(8,128)(2,1)S(1)}, u32[]{:S(2)}, u32[]{:S(2)}) async-start(bf16[8,48,512]{2,1,0:T(8,128)(2,1)} %bitcast.25), calls=%async_computation.3 | async-start | bytes 786432 | tf_op jit(solution)/shard_map/all_to_all | solution.py:165
  117.8 4.4 %fusion.25 = bf16[384,512]{1,0:T(8,128)(2,1)} fusion(bf16[1,2048,512]{2,1,0:T(8,128)(2,1)} %all-gather.5.cloned.1.call-done, f32[384,2048]{1,0:T(8,128)} %fusion.18), kind=kOutput, calls=%fused_computation.34 | convolution fusion | flops 812580864 | bytes 5636096 | tf_op jit(solution)/shard_map/dot_general | solution.py:144
  124.7 4.8 %all-to-all-start.1 = ((bf16[8,48,512]{2,1,0:T(8,128)(2,1)}), bf16[8,48,512]{2,1,0:T(8,128)(2,1)S(1)}, u32[]{:S(2)}, u32[]{:S(2)}) async-start(bf16[8,48,512]{2,1,0:T(8,128)(2,1)} %bitcast.19), calls=%async_computation.1 | async-start | bytes 786432 | tf_op jit(solution)/shard_map/all_to_all | solution.py:162
  130.6 5.9 %all-to-all-done.1 = bf16[8,48,512]{2,1,0:T(8,128)(2,1)S(1)} async-done(((bf16[8,48,512]{2,1,0:T(8,128)(2,1)}), bf16[8,48,512]{2,1,0:T(8,128)(2,1)S(1)}, u32[]{:S(2)}, u32[]{:S(2)}) %all-to-all-start.1) | async-done | bytes 393248 | tf_op jit(solution)/shard_map/all_to_all | solution.py:162
  137.5 49.7 %reduce-scatter.2.cloned.1.call-done = bf16[512,1024]{0,1:T(8,128)(2,1)} async-done(((bf16[2048,1024]{0,1:T(8,128)(2,1)}), bf16[512,1024]{0,1:T(8,128)(2,1)}) %reduce-scatter.2.cloned.1.call-update) | async-done | bytes 1048592 | tf_op jit(solution)/shard_map/reduce_scatter | solution.py:176
  (68 shorter events, 33.1 us)
Async XLA Ops:
  7.2 19.0 %copy-start = (bf16[512,1536]{1,0:T(8,128)(2,1)S(1)}, bf16[512,1536]{1,0:T(8,128)(2,1)}, u32[]{:S(2)}) copy-start(bf16[512,1536]{1,0:T(8,128)(2,1)} %param.12) | copy-start | bytes 4718596
  7.2 75.1 %all-gather.3.cloned.1.call-start = ((), (), s32[]{:S(2)}) async-start(), calls=%async_computation.5 | async-start | bytes 2621440 | tf_op jit(solution)/shard_map/all_gather | solution.py:132
  7.9 92.7 %all-gather.5.cloned.1.call-start = ((), (), s32[]{:S(2)}) async-start(), calls=%async_computation.6 | async-start | bytes 2621440 | tf_op jit(solution)/shard_map/all_gather | solution.py:133
  8.8 7.7 %collective-permute-start = (bf16[4,16,512]{2,1,0:T(8,128)(2,1)S(1)}, bf16[4,16,512]{2,1,0:T(8,128)(2,1)S(1)}, u32[]{:S(2)}, u32[]{:S(2)}) collective-permute-start(bf16[4,16,512]{2,1,0:T(8,128)(2,1)S(1)} %get-tuple-element.20), channel_id=1, source_target_pairs={{0,8},{8,16},{16,24},{1,9},{9,17},{17,25},{2,10},{10,18},{18,26},{... | collective-permute-start | bytes 196616 | tf_op jit(solution)/shard_map/ppermute | solution.py:21
  12.1 5.5 %collective-permute-start.1 = (bf16[4,16,512]{2,1,0:T(8,128)(2,1)S(1)}, bf16[4,16,512]{2,1,0:T(8,128)(2,1)S(1)}, u32[]{:S(2)}, u32[]{:S(2)}) collective-permute-start(bf16[4,16,512]{2,1,0:T(8,128)(2,1)S(1)} %get-tuple-element.19), channel_id=1, source_target_pairs={{8,0},{16,8},{24,16},{9,1},{17,9},{25,17},{10,2},{18,10},{26,18},{... | collective-permute-start | bytes 196616 | tf_op jit(solution)/shard_map/ppermute | solution.py:24
  17.7 7.3 %collective-permute-start.3 = (bf16[24,4,512]{2,1,0:T(4,128)(2,1)S(1)}, bf16[24,4,512]{2,1,0:T(4,128)(2,1)S(1)}, u32[]{:S(2)}, u32[]{:S(2)}) collective-permute-start(bf16[24,4,512]{2,1,0:T(4,128)(2,1)S(1)} %get-tuple-element.18), channel_id=1, source_target_pairs={{1,0},{2,1},{3,2},{4,3},{5,4},{6,5},{7,6},{9,8},{10,9},{11,10},{12... | collective-permute-start | bytes 294920 | tf_op jit(solution)/shard_map/ppermute | solution.py:24
  21.2 4.6 %collective-permute-start.2 = (bf16[24,4,512]{2,1,0:T(4,128)(2,1)S(1)}, bf16[24,4,512]{2,1,0:T(4,128)(2,1)S(1)}, u32[]{:S(2)}, u32[]{:S(2)}) collective-permute-start(bf16[24,4,512]{2,1,0:T(4,128)(2,1)S(1)} %get-tuple-element.17), channel_id=1, source_target_pairs={{0,1},{1,2},{2,3},{3,4},{4,5},{5,6},{6,7},{8,9},{9,10},{10,11},{11... | collective-permute-start | bytes 294920 | tf_op jit(solution)/shard_map/ppermute | solution.py:21
  53.1 2.6 %copy-start.4 = (bf16[9,64,1,16,32]{1,4,3,0,2:T(8,128)(2,1)S(1)}, bf16[9,64,1,16,32]{1,4,3,0,2:T(8,128)(2,1)}, u32[]{:S(2)}) copy-start(bf16[9,64,1,16,32]{1,4,3,0,2:T(8,128)(2,1)} %copy.25) | copy-start | bytes 1769476
  59.4 4.0 %copy-start.5 = (bf16[512,512]{1,0:T(8,128)(2,1)S(1)}, bf16[512,512]{1,0:T(8,128)(2,1)}, u32[]{:S(2)}) copy-start(bf16[512,512]{1,0:T(8,128)(2,1)} %param.13) | copy-start | bytes 1572868
  59.4 4.6 %copy-start.3 = (bf16[16,16,512]{2,1,0:T(8,128)(2,1)S(1)}, bf16[16,16,512]{2,1,0:T(8,128)(2,1)}, u32[]{:S(2)}) copy-start(bf16[16,16,512]{2,1,0:T(8,128)(2,1)} %param.8) | copy-start | bytes 786436
  63.2 7.3 %copy-start.7 = (f32[16,16]{1,0:T(8,128)S(1)}, f32[16,16]{1,0:T(8,128)}, u32[]{:S(2)}) copy-start(f32[16,16]{1,0:T(8,128)} %param.9) | copy-start | bytes 3076
  63.2 7.4 %copy-start.6 = (bf16[16,16,512]{2,1,0:T(8,128)(2,1)S(1)}, bf16[16,16,512]{2,1,0:T(8,128)(2,1)}, u32[]{:S(2)}) copy-start(bf16[16,16,512]{2,1,0:T(8,128)(2,1)} %param.11) | copy-start | bytes 786436
  65.3 12.1 %all-to-all-start = ((bf16[8,48,512]{2,1,0:T(8,128)(2,1)}), bf16[8,48,512]{2,1,0:T(8,128)(2,1)S(1)}, u32[]{:S(2)}, u32[]{:S(2)}) async-start(bf16[8,48,512]{2,1,0:T(8,128)(2,1)} %bitcast.15), calls=%async_computation | async-start | bytes 786432 | tf_op jit(solution)/shard_map/all_to_all | solution.py:160
  77.4 11.7 %all-to-all-start.2 = ((bf16[8,48,512]{2,1,0:T(8,128)(2,1)}), bf16[8,48,512]{2,1,0:T(8,128)(2,1)S(1)}, u32[]{:S(2)}, u32[]{:S(2)}) async-start(bf16[8,48,512]{2,1,0:T(8,128)(2,1)} %bitcast.23), calls=%async_computation.2 | async-start | bytes 786432 | tf_op jit(solution)/shard_map/all_to_all | solution.py:163
  82.2 104.9 %reduce-scatter.2.cloned.1.call-start = ((), (), s32[]{:S(2)}) async-start(), calls=%async_computation.7 | async-start | bytes 5242880 | tf_op jit(solution)/shard_map/reduce_scatter | solution.py:176
  105.4 1.6 copy-start.2
  112.8 11.9 %all-to-all-start.3 = ((bf16[8,48,512]{2,1,0:T(8,128)(2,1)}), bf16[8,48,512]{2,1,0:T(8,128)(2,1)S(1)}, u32[]{:S(2)}, u32[]{:S(2)}) async-start(bf16[8,48,512]{2,1,0:T(8,128)(2,1)} %bitcast.25), calls=%async_computation.3 | async-start | bytes 786432 | tf_op jit(solution)/shard_map/all_to_all | solution.py:165
  124.7 11.7 %all-to-all-start.1 = ((bf16[8,48,512]{2,1,0:T(8,128)(2,1)}), bf16[8,48,512]{2,1,0:T(8,128)(2,1)S(1)}, u32[]{:S(2)}, u32[]{:S(2)}) async-start(bf16[8,48,512]{2,1,0:T(8,128)(2,1)} %bitcast.19), calls=%async_computation.1 | async-start | bytes 786432 | tf_op jit(solution)/shard_map/all_to_all | solution.py:162
  188.6 5.1 %copy-start.1 = (bf16[512,1536]{1,0:T(8,128)(2,1)S(1)}, bf16[512,1536]{1,0:T(8,128)(2,1)}, u32[]{:S(2)}) copy-start(bf16[512,1536]{1,0:T(8,128)(2,1)} %param.12) | copy-start | bytes 4718596
Sparse Core Ops, SparseCore 0:
  9.6 44.9 all-gather.2
  56.1 44.4 all-gather.4
  109.6 77.4 reduce-scatter.1
where the time goes:
time: 203 us; the launch traced here: 200 us
  waiting for transfers between devices  74.5 us (37%)
  local copies, waits for them, and re-layouts  38.3 us (19%)
  starting transfers between devices  31.6 us (16%)
  matrix products  30.4 us (15%)
  between operations  14.1 us (7%)
  other arithmetic  11.3 us (6%)
    reduce_scatter x1, waiting for transfers between devices, per_device(): lax.psum_scatter(jnp.concatenate([up_part, down_part], axis=1).astype(jnp...  49.7 us
    unnamed x23, local copies, waits for them, and re-layouts  16.5 us
    slice x1, local copies, waits for them, and re-layouts, window_attend(): blocks[:, :, 2]  6.87 us
    all_gather x1, waiting for transfers between devices, per_device(): lax.all_gather(w_down, 'rep', axis=1, tiled=True)  6.67 us
    reshape x1, local copies, waits for them, and re-layouts, window_attend(): blocks = blocks.reshape(win_rows * win_cols, cells, 3, HEADS, head_size)  6.6 us
    ppermute x2, starting transfers between devices, padded(): lax.ppermute(lax.slice_in_dim(block, block.shape[dim] - width, None, axis...  6.22 us
    all_to_all x1, waiting for transfers between devices, per_device(): lax.all_to_all(expert_out, 'exp', split_axis=0, concat_axis=0, tiled=True)  5.86 us
    all_to_all x1, waiting for transfers between devices, per_device(): lax.all_to_all(to_slots(mixed), 'exp', split_axis=0, concat_axis=0, tiled...  5.65 us
  transfers between devices with their start and end apart: 11, of which 7 were waited for; matrix products, arithmetic and copies ran while one was open for 32% of the time, Pallas kernels for 0%

commit v1 on v0

--- a/solution.py
+++ b/solution.py
@@ -3,6 +3,8 @@
 import jax
 import jax.numpy as jnp
 from jax import lax
+from jax.experimental import pallas as pl
+from jax.experimental.pallas import tpu as pltpu
 from jax.sharding import PartitionSpec as P
 
 HEADS = 16
@@ -76,6 +78,280 @@
     return context.reshape(ext_rows, ext_cols, feature)
 
 
+def enter(ring, ranks):
+    barrier = pltpu.get_barrier_semaphore()
+    me, row = lax.axis_index("exp"), lax.axis_index("rep")
+
+    def greet(step, carry):
+        pl.semaphore_signal(barrier, device_id={"exp": lax.rem(me + step, ring)})
+        return carry
+
+    lax.fori_loop(1, ring, greet, 0)
+
+    @pl.when(row > 0)
+    def _():
+        pl.semaphore_signal(barrier, device_id={"rep": row - 1})
+
+    @pl.when(row < ranks - 1)
+    def _():
+        pl.semaphore_signal(barrier, device_id={"rep": row + 1})
+
+    below = (row + ranks - 1) // ranks
+    above = (2 * ranks - 2 - row) // ranks
+    pl.semaphore_wait(barrier, ring - 1 + below + above)
+
+
+def swap_start(ring, cap, source, target, send_sem, recv_sem):
+    me = lax.axis_index("exp")
+    mine = pl.ds(pl.multiple_of(me * cap, 16), cap)
+
+    def send(step, carry):
+        peer = lax.rem(me + step, ring)
+        pltpu.make_async_remote_copy(
+            src_ref=source.at[pl.ds(pl.multiple_of(peer * cap, 16), cap)],
+            dst_ref=target.at[mine],
+            send_sem=send_sem,
+            recv_sem=recv_sem,
+            device_id={"exp": peer},
+        ).start()
+        return carry
+
+    lax.fori_loop(1, ring, send, 0)
+    pltpu.make_async_copy(source.at[mine], target.at[mine], recv_sem).start()
+
+
+def await_bytes(ref, sem):
+    pltpu.make_async_copy(ref, ref, sem).wait()
+
+
+def spread_kernel(
+    count, ring, ranks, cap, values, placers, out, held, slots, z_send, z_recv, a_send, a_recv
+):
+    row = lax.axis_index("rep")
+    enter(ring, ranks)
+
+    def pass_on(t, origin, source, side):
+        pltpu.make_async_remote_copy(
+            src_ref=source,
+            dst_ref=held.at[t, origin],
+            send_sem=z_send.at[t, origin, (side + 1) // 2],
+            recv_sem=z_recv.at[t, origin],
+            device_id={"rep": row + side},
+        ).start()
+
+    def dispatch(t, origin, tokens):
+        slots[t, origin] = jnp.dot(
+            placers[origin], tokens, preferred_element_type=jnp.float32
+        ).astype(jnp.bfloat16)
+        swap_start(
+            ring, cap, slots.at[t, origin], out.at[t, origin], a_send.at[t, origin], a_recv.at[t, origin]
+        )
+
+    for t in range(count):
+
+        @pl.when(row < ranks - 1)
+        def _():
+            pass_on(t, row, values[t], 1)
+
+        @pl.when(row > 0)
+        def _():
+            pass_on(t, row, values[t], -1)
+
+    for t in range(count):
+        dispatch(t, row, values[t][...])
+
+    def step(k, carry):
+        for t in range(count):
+            for side in (1, -1):
+                origin = row - side * k
+
+                @pl.when((origin >= 0) & (origin < ranks))
+                def _():
+                    await_bytes(held.at[t, origin], z_recv.at[t, origin])
+                    onward = row + side
+
+                    @pl.when((onward >= 0) & (onward < ranks))
+                    def _():
+                        pass_on(t, origin, held.at[t, origin], side)
+
+                    dispatch(t, origin, held[t, origin])
+
+        return carry
+
+    lax.fori_loop(1, ranks, step, 0)
+
+    def finish(origin, carry):
+        for t in range(count):
+            await_bytes(out.at[t, origin], a_recv.at[t, origin])
+            sent = slots.at[t, origin, pl.ds(0, (ring - 1) * cap)]
+            await_bytes(sent, a_send.at[t, origin])
+
+            @pl.when((origin <= row) & (row < ranks - 1))
+            def _():
+                await_bytes(held.at[t, origin], z_send.at[t, origin, 1])
+
+            @pl.when((origin >= row) & (row > 0))
+            def _():
+                await_bytes(held.at[t, origin], z_send.at[t, origin, 0])
+
+        return carry
+
+    lax.fori_loop(0, ranks, finish, 0)
+
+
+def collect_kernel(
+    count, ring, ranks, cap, parts, placers, out, back, sums, z_send, z_recv, a_send, a_recv
+):
+    row = lax.axis_index("rep")
+    enter(ring, ranks)
+
+    def launch(t, target):
+        swap_start(
+            ring, cap, parts[t].at[target], back.at[t, target], a_send.at[t, target], a_recv.at[t, target]
+        )
+
+    def ahead(step, carry):
+        k = ranks - step
+        for t in range(count):
+            for side in (1, -1):
+                target = row + side * k
+
+                @pl.when((target >= 0) & (target < ranks))
+                def _():
+                    launch(t, target)
+
+        return carry
+
+    lax.fori_loop(1, ranks, ahead, 0)
+    for t in range(count):
+        launch(t, row)
+
+    def placed(t, target):
+        await_bytes(back.at[t, target], a_recv.at[t, target])
+        return jnp.dot(placers[target], back[t, target], preferred_element_type=jnp.float32)
+
+    def step(index, carry):
+        k = ranks - index
+        for t in range(count):
+            for side in (1, -1):
+                target = row + side * k
+
+                @pl.when((target >= 0) & (target < ranks))
+                def _():
+                    own = placed(t, target)
+                    behind = row - side
+                    first = (behind < 0) | (behind >= ranks)
+
+                    @pl.when(first)
+                    def _():
+                        sums[t, target] = own.astype(jnp.bfloat16)
+
+                    @pl.when(jnp.logical_not(first))
+                    def _():
+                        await_bytes(sums.at[t, target], z_recv.at[t, target])
+                        total = own + sums[t, target].astype(jnp.float32)
+                        sums[t, target] = total.astype(jnp.bfloat16)
+
+                    final = ranks if side < 0 else target
+                    place = jnp.where(k == 1, final, target)
+                    pltpu.make_async_remote_copy(
+                        src_ref=sums.at[t, target],
+                        dst_ref=sums.at[t, place],
+                        send_sem=z_send.at[t, target],
+                        recv_sem=z_recv.at[t, place],
+                        device_id={"rep": row + side},
+                    ).start()
+
+        return carry
+
+    lax.fori_loop(1, ranks, step, 0)
+    for t in range(count):
+        out[t] = placed(t, row)
+
+        @pl.when(row > 0)
+        def _():
+            await_bytes(sums.at[t, row], z_recv.at[t, row])
+            out[t] += sums[t, row].astype(jnp.float32)
+
+        @pl.when(row < ranks - 1)
+        def _():
+            await_bytes(sums.at[t, ranks], z_recv.at[t, ranks])
+            out[t] += sums[t, ranks].astype(jnp.float32)
+
+    def finish(target, carry):
+        for t in range(count):
+            sent = back.at[t, target, pl.ds(0, (ring - 1) * cap)]
+            await_bytes(sent, a_send.at[t, target])
+
+            @pl.when(target != row)
+            def _():
+                await_bytes(sums.at[t, target], z_send.at[t, target])
+
+        return carry
+
+    lax.fori_loop(0, ranks, finish, 0)
+
+
+def in_vmem(amount):
+    return [pl.BlockSpec(memory_space=pltpu.VMEM)] * amount
+
+
+def spread(values, placers, ring, ranks, cap):
+    count = len(values)
+    tok, feature = values[0].shape
+
+    def body(*refs):
+        spread_kernel(count, ring, ranks, cap, refs[:count], *refs[count:])
+
+    rows = ring * cap
+    return pl.pallas_call(
+        body,
+        name="spread",
+        out_shape=jax.ShapeDtypeStruct((count, ranks, rows, feature), jnp.bfloat16),
+        in_specs=in_vmem(count + 1),
+        out_specs=pl.BlockSpec(memory_space=pltpu.VMEM),
+        scratch_shapes=[
+            pltpu.VMEM((count, ranks, tok, feature), jnp.bfloat16),
+            pltpu.VMEM((count, ranks, rows, feature), jnp.bfloat16),
+            pltpu.SemaphoreType.DMA((count, ranks, 2)),
+            pltpu.SemaphoreType.DMA((count, ranks)),
+            pltpu.SemaphoreType.DMA((count, ranks)),
+            pltpu.SemaphoreType.DMA((count, ranks)),
+        ],
+        compiler_params=pltpu.CompilerParams(
+            collective_id=0, has_side_effects=True, vmem_limit_bytes=60 << 20
+        ),
+    )(*values, placers)
+
+
+def collect(parts, placers, ring, ranks, cap):
+    count = len(parts)
+    rows, feature = parts[0].shape[1:]
+    tok = placers.shape[1]
+
+    def body(*refs):
+        collect_kernel(count, ring, ranks, cap, refs[:count], *refs[count:])
+
+    return pl.pallas_call(
+        body,
+        name="collect",
+        out_shape=jax.ShapeDtypeStruct((count, tok, feature), jnp.float32),
+        in_specs=in_vmem(count + 1),
+        out_specs=pl.BlockSpec(memory_space=pltpu.VMEM),
+        scratch_shapes=[
+            pltpu.VMEM((count, ranks, rows, feature), jnp.bfloat16),
+            pltpu.VMEM((count, ranks + 1, tok, feature), jnp.bfloat16),
+            pltpu.SemaphoreType.DMA((count, ranks)),
+            pltpu.SemaphoreType.DMA((count, ranks + 1)),
+            pltpu.SemaphoreType.DMA((count, ranks)),
+            pltpu.SemaphoreType.DMA((count, ranks)),
+        ],
+        compiler_params=pltpu.CompilerParams(
+            collective_id=1, has_side_effects=True, vmem_limit_bytes=60 << 20
+        ),
+    )(*parts, placers)
+
+
 def per_device(tokens, gate, route, cotangent, w_qkv, w_proj, w_up, w_down):
     tile_rows, tile_cols, feature = tokens.shape
     tok_count = tile_rows * tile_cols
@@ -102,91 +378,54 @@
     flat_tokens = tokens.reshape(tok_count, feature)
     mixed = (flat_tokens.astype(jnp.float32) + layer_norm(attended)).astype(jnp.bfloat16)
     experts = lax.axis_size("exp")
+    ranks = lax.axis_size("rep")
     capacity = max(2, 3 * tok_count // (2 * experts))
+    capacity = -(-capacity // 16) * 16
+    slot_count = experts * capacity
     chosen = route.reshape(tok_count)
     matches = (chosen[:, None] == jnp.arange(experts, dtype=jnp.int32)[None, :]).astype(jnp.int32)
     position = jnp.sum(matches * (jnp.cumsum(matches, axis=0) - 1), axis=1)
-    target = chosen * capacity + position
-    placer = (target[:, None] == jnp.arange(experts * capacity, dtype=jnp.int32)[None, :]).astype(
-        jnp.bfloat16
-    )
+    targets = lax.all_gather(chosen * capacity + position, "rep")
+    slot_ids = jnp.arange(slot_count, dtype=jnp.int32)
+    to_slots = (slot_ids[None, :, None] == targets[:, None, :]).astype(jnp.bfloat16)
+    from_slots = (targets[:, :, None] == slot_ids[None, None, :]).astype(jnp.bfloat16)
     gate_rows = gate.reshape(tok_count)
     upstream = (
         gate_rows[:, None] * cotangent.reshape(tok_count, feature).astype(jnp.float32)
     ).astype(jnp.bfloat16)
-
-    def to_slots(values):
-        placed = lax.dot_general(
-            placer, values, (((0,), (0,)), ((), ())), preferred_element_type=jnp.float32
-        )
-        return placed.astype(jnp.bfloat16).reshape(experts, capacity, feature)
-
-    def from_slots(slot_values):
-        return jnp.dot(
-            placer,
-            slot_values.reshape(experts * capacity, feature),
-            preferred_element_type=jnp.float32,
-        )
-
-    up_whole, down_whole = (
-        lax.all_gather(w_up, "rep", axis=1, tiled=True),
-        lax.all_gather(w_down, "rep", axis=1, tiled=True),
-    )
-    up_mat = up_whole[0]
-    down_mat = down_whole[0]
-
-    def forward(sent_x):
-        slot_rows = sent_x.reshape(-1, feature)
-        pre_act = lax.dot_general(
-            slot_rows, up_mat, (((1,), (1,)), ((), ())), preferred_element_type=jnp.float32
-        )
-        hidden = gelu_tanh(pre_act).astype(jnp.bfloat16)
-        expert_out = jnp.dot(hidden, down_mat, preferred_element_type=jnp.float32).astype(
-            jnp.bfloat16
-        )
-        return (slot_rows, pre_act, hidden, expert_out.reshape(-1, capacity, feature))
-
-    def backward(pre_act, sent_g):
-        slot_grads = sent_g.reshape(-1, feature)
-        hidden_grad = lax.dot_general(
-            slot_grads, down_mat, (((1,), (1,)), ((), ())), preferred_element_type=jnp.float32
-        )
-        pre_grad = (hidden_grad * gelu_slope(pre_act)).astype(jnp.bfloat16)
-        input_slots = jnp.dot(pre_grad, up_mat, preferred_element_type=jnp.float32).astype(
-            jnp.bfloat16
-        )
-        return (slot_grads, pre_grad, input_slots.reshape(-1, capacity, feature))
-
-    sent_x = lax.all_to_all(to_slots(mixed), "exp", split_axis=0, concat_axis=0, tiled=True)
-    slot_rows, pre_act, hidden, expert_out = forward(sent_x)
-    back_out = lax.all_to_all(expert_out, "exp", split_axis=0, concat_axis=0, tiled=True)
-    sent_g = lax.all_to_all(to_slots(upstream), "exp", split_axis=0, concat_axis=0, tiled=True)
-    slot_grads, pre_grad, input_slots = backward(pre_act, sent_g)
-    back_grad = lax.all_to_all(input_slots, "exp", split_axis=0, concat_axis=0, tiled=True)
-    layer_out = (mixed.astype(jnp.float32) + gate_rows[:, None] * from_slots(back_out)).astype(
-        jnp.bfloat16
-    )
-    input_grad = from_slots(back_grad).astype(jnp.bfloat16)
-    up_part = lax.dot_general(
+    gathered = spread((upstream, mixed), to_slots, experts, ranks, capacity)
+    slot_grads = gathered[0].reshape(-1, feature)
+    slot_rows = gathered[1].reshape(-1, feature)
+    up_mat = w_up[0]
+    down_mat = w_down[0]
+    pre_act = lax.dot_general(
+        slot_rows, up_mat, (((1,), (1,)), ((), ())), preferred_element_type=jnp.float32
+    )
+    hidden = gelu_tanh(pre_act).astype(jnp.bfloat16)
+    expert_out = jnp.dot(hidden, down_mat, preferred_element_type=jnp.float32).astype(jnp.bfloat16)
+    hidden_grad = lax.dot_general(
+        slot_grads, down_mat, (((1,), (1,)), ((), ())), preferred_element_type=jnp.float32
+    )
+    pre_grad = (hidden_grad * gelu_slope(pre_act)).astype(jnp.bfloat16)
+    input_slots = jnp.dot(pre_grad, up_mat, preferred_element_type=jnp.float32).astype(jnp.bfloat16)
+    shape = (ranks, slot_count, feature)
+    returned = collect(
+        (expert_out.reshape(shape), input_slots.reshape(shape)), from_slots, experts, ranks, capacity
+    )
+    layer_out = (mixed.astype(jnp.float32) + gate_rows[:, None] * returned[0]).astype(jnp.bfloat16)
+    input_grad = returned[1].astype(jnp.bfloat16)
+    average_factor = 1.0 / ranks
+    grad_up = lax.dot_general(
         pre_grad, slot_rows, (((0,), (0,)), ((), ())), preferred_element_type=jnp.float32
     )
-    down_part = lax.dot_general(
+    grad_down = lax.dot_general(
         hidden, slot_grads, (((0,), (0,)), ((), ())), preferred_element_type=jnp.float32
     )
-    summed = lax.psum_scatter(
-        jnp.concatenate([up_part, down_part], axis=1).astype(jnp.bfloat16),
-        "rep",
-        scatter_dimension=0,
-        tiled=True,
-    ).astype(jnp.float32)
-    grad_up_rows = summed[:, :feature]
-    grad_down_rows = summed[:, feature:]
-    average_factor = 1.0 / lax.axis_size("rep")
     return (
         layer_out.reshape(tile_rows, tile_cols, feature),
         input_grad.reshape(tile_rows, tile_cols, feature),
-        (grad_up_rows * average_factor)[None],
-        (grad_down_rows * average_factor)[None],
+        (grad_up * average_factor)[None],
+        (grad_down * average_factor)[None],
     )
 
 

time: 203 us -> 190 us (0.936); the launches traced: 200 us -> 189 us
  Pallas kernels: 0 us -> 95.1 us
  waiting for transfers between devices: 74.5 us -> 4.73 us
  starting transfers between devices: 31.6 us -> 13.5 us
  matrix products: 30.4 us -> 16.6 us
  between operations: 14.1 us -> 0.92 us
  blocking collectives: 0 us -> 6.21 us
    pallas_call x0 -> x2, Pallas kernels: none -> 95.1 us  [the longest x1 53.1 us: collect(): pl.pallas_call(body, name='collect', out_shape=jax.ShapeDtypeStruct((coun...]
    reduce_scatter x1 -> x0, waiting for transfers between devices: 49.7 us -> none  [per_device(): lax.psum_scatter(jnp.concatenate([up_part, down_part], axis=1).astype(jnp...]
    all_to_all x4 -> x0, starting transfers between devices: 19.7 us -> none  [the longest x1 5.2 us: per_device(): lax.all_to_all(to_slots(mixed), 'exp', split_axis=0, concat_axis=0, tiled...]
    all_to_all x4 -> x0, waiting for transfers between devices: 16.6 us -> none  [the longest x1 5.86 us: per_device(): lax.all_to_all(expert_out, 'exp', split_axis=0, concat_axis=0, tiled=True)]
    dot_general x8 -> x4, matrix products: 21.2 us -> 7.94 us  [the longest x1 2.39 us: per_device(): lax.dot_general(slot_grads, down_mat, (((1,), (1,)), ((), ())), preferred...]
    all_gather x2 -> x0, waiting for transfers between devices: 6.67 us -> none  [the longest x1 6.67 us: per_device(): lax.all_gather(w_down, 'rep', axis=1, tiled=True)]
    all_gather x0 -> x1, blocking collectives: none -> 6.21 us  [per_device(): targets = lax.all_gather(chosen * capacity + position, 'rep')]
    ppermute x2, waiting for transfers between devices: 0.01 us -> 4.72 us  [padded(): lax.ppermute(lax.slice_in_dim(block, 0, width, axis=dim), axis, backward)]
  transfers between devices with their start and end apart: 11 -> 4, of which waited for: 7 -> 1; matrix products, arithmetic and copies ran while one was open for 32% -> 5% of each run, Pallas kernels for 0% -> 0%
where the time goes in v1:
time: 190 us; the launch traced here: 189 us
  Pallas kernels  95.1 us (50%)
  local copies, waits for them, and re-layouts  39.8 us (21%)
  matrix products  16.6 us (9%)
  starting transfers between devices  13.5 us (7%)
  other arithmetic  12.6 us (7%)
  blocking collectives  6.21 us (3%)
  waiting for transfers between devices  4.73 us (2%)
    pallas_call x1, Pallas kernels, collect(): pl.pallas_call(body, name='collect', out_shape=jax.ShapeDtypeStruct((coun...  53.1 us
    pallas_call x1, Pallas kernels, spread(): pl.pallas_call(body, name='spread', out_shape=jax.ShapeDtypeStruct((count...  41.9 us
    unnamed x20, local copies, waits for them, and re-layouts  13.2 us
    ppermute x2, starting transfers between devices, padded(): lax.ppermute(lax.slice_in_dim(block, block.shape[dim] - width, None, axis...  9.46 us
    slice x1, local copies, waits for them, and re-layouts, window_attend(): blocks[:, :, 2]  6.86 us
    reshape x1, local copies, waits for them, and re-layouts, window_attend(): blocks = blocks.reshape(win_rows * win_cols, cells, 3, HEADS, head_size)  6.6 us
    all_gather x1, blocking collectives, per_device(): targets = lax.all_gather(chosen * capacity + position, 'rep')  6.21 us
    ppermute x2, waiting for transfers between devices, padded(): lax.ppermute(lax.slice_in_dim(block, 0, width, axis=dim), axis, backward)  4.72 us
  transfers between devices with their start and end apart: 4, of which 1 were waited for; matrix products, arithmetic and copies ran while one was open for 5% of the time, Pallas kernels for 0%

profile of v1, /device:TPU:11, one launch (start us, length us, event | category | flops | bytes accessed | tf_op | source)
XLA Modules:
  0.0 189.4 jit_solution(8982942867356437881)
XLA Ops:
  1.6 3.2 %collective-permute-start = (bf16[4,16,512]{2,1,0:T(8,128)(2,1)S(1)}, bf16[4,16,512]{2,1,0:T(8,128)(2,1)S(1)}, u32[]{:S(2)}, u32[]{:S(2)}) collective-permute-start(bf16[4,16,512]{2,1,0:T(8,128)(2,1)S(1)} %get-tuple-element.12), channel_id=1, source_target_pairs={{0,8},{8,16},{16,24},{1,9},{9,17},{17,25},{2,10},{10,18},{18,26},{... | collective-permute-start | bytes 196616 | tf_op jit(solution)/shard_map/ppermute | solution.py:23
  4.9 2.1 %collective-permute-start.1 = (bf16[4,16,512]{2,1,0:T(8,128)(2,1)S(1)}, bf16[4,16,512]{2,1,0:T(8,128)(2,1)S(1)}, u32[]{:S(2)}, u32[]{:S(2)}) collective-permute-start(bf16[4,16,512]{2,1,0:T(8,128)(2,1)S(1)} %get-tuple-element.11), channel_id=1, source_target_pairs={{8,0},{16,8},{24,16},{9,1},{17,9},{25,17},{10,2},{18,10},{26,18},{... | collective-permute-start | bytes 196616 | tf_op jit(solution)/shard_map/ppermute | solution.py:26
  9.9 6.2 %all-gather = s32[4,1,256]{2,1,0:T(1,128)S(1)} all-gather(s32[1,1,256]{2,1,0:T(1,128)S(1)} %fusion.41), channel_id=1, replica_groups=mesh['rep'=4,'exp'=8] {'rep'}, dimensions={0}, use_global_device_ids=true | all-gather | bytes 5120 | tf_op jit(solution)/shard_map/all_gather | solution.py:388
  22.0 6.3 %collective-permute-start.2 = (bf16[24,4,512]{2,1,0:T(4,128)(2,1)S(1)}, bf16[24,4,512]{2,1,0:T(4,128)(2,1)S(1)}, u32[]{:S(2)}, u32[]{:S(2)}) collective-permute-start(bf16[24,4,512]{2,1,0:T(4,128)(2,1)S(1)} %get-tuple-element.9), channel_id=1, source_target_pairs={{0,1},{1,2},{2,3},{3,4},{4,5},{5,6},{6,7},{8,9},{9,10},{10,11},{11... | collective-permute-start | bytes 294920 | tf_op jit(solution)/shard_map/ppermute | solution.py:23
  28.2 1.9 %collective-permute-start.3 = (bf16[24,4,512]{2,1,0:T(4,128)(2,1)S(1)}, bf16[24,4,512]{2,1,0:T(4,128)(2,1)S(1)}, u32[]{:S(2)}, u32[]{:S(2)}) collective-permute-start(bf16[24,4,512]{2,1,0:T(4,128)(2,1)S(1)} %get-tuple-element.10), channel_id=1, source_target_pairs={{1,0},{2,1},{3,2},{4,3},{5,4},{6,5},{7,6},{9,8},{10,9},{11,10},{12... | collective-permute-start | bytes 294920 | tf_op jit(solution)/shard_map/ppermute | solution.py:26
  30.4 4.7 %collective-permute-done.3 = bf16[24,4,512]{2,1,0:T(4,128)(2,1)S(1)} collective-permute-done((bf16[24,4,512]{2,1,0:T(4,128)(2,1)S(1)}, bf16[24,4,512]{2,1,0:T(4,128)(2,1)S(1)}, u32[]{:S(2)}, u32[]{:S(2)}) %collective-permute-start.3) | collective-permute-done | bytes 98336 | tf_op jit(solution)/shard_map/ppermute | solution.py:26
  36.7 6.6 %reshape.127 = bf16[9,64,3,16,32]{4,3,2,1,0:T(8,128)(2,1)} reshape(bf16[3,3,8,8,1536]{4,3,2,1,0:T(8,128)(2,1)S(1)} %bitcast.87) | data formatting | bytes 3538944 | tf_op jit(solution)/shard_map/reshape | solution.py:59
  43.3 6.9 %fusion.44 = (bf16[9,64,1,16,32]{4,3,2,1,0:T(8,128)(2,1)}, bf16[9,64,1,16,32]{4,3,2,1,0:T(8,128)(2,1)}, bf16[9,64,1,16,32]{4,3,2,1,0:T(8,128)(2,1)}) fusion(bf16[9,64,3,16,32]{4,3,2,1,0:T(8,128)(2,1)} %reshape.127), kind=kLoop, calls=%fused_computation.78 | loop fusion | bytes 3538944 | tf_op jit(solution)/shard_map/slice | solution.py:73
  50.1 3.5 %copy.30 = bf16[9,64,1,16,32]{1,4,3,0,2:T(8,128)(2,1)S(1)} copy(bf16[9,64,1,16,32]{4,3,2,1,0:T(8,128)(2,1)} %get-tuple-element.5) | data formatting | bytes 1179648
  53.6 4.3 %copy.31 = bf16[9,64,1,16,32]{1,4,3,0,2:T(8,128)(2,1)} copy(bf16[9,64,1,16,32]{4,3,2,1,0:T(8,128)(2,1)} %get-tuple-element.6) | data formatting | bytes 1179648
  57.9 4.3 %copy.29 = bf16[9,64,1,16,32]{1,4,3,0,2:T(8,128)(2,1)} copy(bf16[9,64,1,16,32]{4,3,2,1,0:T(8,128)(2,1)} %get-tuple-element.4) | data formatting | bytes 1179648
  62.3 2.1 %fusion.18 = f32[9,16,64,64]{2,3,1,0:T(8,128)S(1)} fusion(bf16[9,64,1,16,32]{1,4,3,0,2:T(8,128)(2,1)} %copy.31, bf16[9,64,1,16,32]{1,4,3,0,2:T(8,128)(2,1)S(1)} %copy.30), kind=kOutput, calls=%fused_computation.33 | convolution fusion | flops 37748736 | bytes 3538944 | tf_op jit(solution)/shard_map/wqhd,wkhd->whqk/dot_general | solution.py:65
  64.4 2.6 %fusion.48 = (f32[9,16,64]{2,1,0:T(8,128)S(1)}, f32[9,16,64,64]{2,3,1,0:T(8,128)S(1)}) fusion(f32[9,16,64,64]{2,3,1,0:T(8,128)S(1)} %fusion.18, pred[9,64]{1,0:T(8,128)(4,1)S(1)} %and.40), kind=kOutput, calls=%fused_computation.82 | output fusion | flops 3539007 | bytes 4756032 | tf_op jit(solution)/shard_map/sub | solution.py:70
  67.8 3.0 %copy.25 = bf16[9,64,16,32]{3,2,1,0:T(8,128)(2,1)} copy(bf16[9,64,16,32]{1,3,2,0:T(8,128)(2,1)S(1)} %fusion.15) | data formatting | bytes 1179648 | tf_op jit(solution)/shard_map/convert_element_type | solution.py:74
  70.7 3.8 %reshape.128 = bf16[3,3,8,8,512]{4,3,2,1,0:T(8,128)(2,1)S(1)} reshape(bf16[9,64,16,32]{3,2,1,0:T(8,128)(2,1)} %copy.25) | data formatting | bytes 1179648 | tf_op jit(solution)/shard_map/reshape | solution.py:75
  76.2 41.9 %spread.1 = bf16[2,4,384,512]{3,2,1,0:T(8,128)(2,1)} custom-call(bf16[256,512]{1,0:T(8,128)(2,1)} %fusion.22.refs_0_, bf16[256,512]{1,0:T(8,128)(2,1)} %fusion.23.refs_1_, bf16[4,384,256]{2,1,0:T(8,128)(2,1)} %fusion.12.refs_2_), custom_call_target="tpu_custom_call" | custom-call | tf_op jit(solution)/shard_map/spread/pallas_call | solution.py:307
  118.1 2.1 %fusion.45 = (bf16[1,4,384,512]{3,2,1,0:T(8,128)(2,1)S(1)}, bf16[1,4,384,512]{3,2,1,0:T(8,128)(2,1)S(1)}) fusion(bf16[2,4,384,512]{3,2,1,0:T(8,128)(2,1)} %spread.1), kind=kLoop, calls=%fused_computation.79 | loop fusion | bytes 6291456 | tf_op jit(solution)/shard_map/slice | solution.py:397
  121.3 2.3 %fusion.16 = f32[1,512,512]{2,1,0:T(8,128)} fusion(bf16[1536,512]{1,0:T(8,128)(2,1)S(1)} %bitcast.92, f32[1536,512]{1,0:T(8,128)S(1)} %fusion.29), kind=kOutput, calls=%fused_computation.30 | convolution fusion | flops 812646400 | bytes 5767168 | tf_op jit(solution)/shard_map/dot_general | solution.py:421
  123.7 2.4 %fusion.7 = bf16[1536,512]{1,0:T(8,128)(2,1)S(1)} fusion(f32[1536,512]{1,0:T(8,128)S(1)} %fusion.29, bf16[1536,512]{1,0:T(8,128)(2,1)S(1)} %bitcast.93, bf16[1,512,512]{2,1,0:T(8,128)(2,1)S(1)} %copy-done.6), kind=kOutput, calls=%fused_computation.17 | convolution fusion | flops 820248576 | bytes 6815744 | tf_op jit(solution)/shard_map/dot_general | solution.py:406
  126.1 2.0 %fusion.17 = f32[1,512,512]{2,1,0:T(8,128)} fusion(bf16[1536,512]{1,0:T(8,128)(2,1)S(1)} %fusion.7, bf16[1536,512]{1,0:T(8,128)(2,1)S(1)} %bitcast.86), kind=kOutput, calls=%fused_computation.32 | convolution fusion | flops 805568512 | bytes 4194304 | tf_op jit(solution)/shard_map/dot_general | solution.py:418
  128.0 2.1 %convolution_convert_fusion.1 = bf16[1536,512]{1,0:T(8,128)(2,1)} fusion(bf16[1536,512]{1,0:T(8,128)(2,1)S(1)} %fusion.7, bf16[1,512,512]{2,1,0:T(8,128)(2,1)S(1)} %copy-done.4), kind=kOutput, calls=%fused_computation.15 | convolution fusion | flops 806092800 | bytes 3670016 | tf_op jit(solution)/shard_map/dot_general | solution.py:410
  130.2 2.4 %convolution_convert_fusion.2 = bf16[1536,512]{1,0:T(8,128)(2,1)} fusion(bf16[1,512,512]{2,1,0:T(8,128)(2,1)S(1)} %copy-done.6, f32[1536,512]{1,0:T(8,128)S(1)} %fusion.29), kind=kOutput, calls=%fused_computation.16 | convolution fusion | flops 813170688 | bytes 5242880 | tf_op jit(solution)/shard_map/dot_general | solution.py:405
  132.5 53.1 %collect.1 = f32[2,256,512]{2,1,0:T(8,128)} custom-call(bf16[4,384,512]{2,1,0:T(8,128)(2,1)} %bitcast.91, bf16[4,384,512]{2,1,0:T(8,128)(2,1)} %bitcast.90, bf16[4,256,384]{2,1,0:T(8,128)(2,1)} %fusion.13.refs_2_), custom_call_target="tpu_custom_call" | custom-call | tf_op jit(solution)/shard_map/collect/pallas_call | solution.py:335
  185.7 1.9 fusion.25
  (50 shorter events, 16.7 us)
Async XLA Ops:
  0.6 34.8 %copy-start = (bf16[512,1536]{1,0:T(8,128)(2,1)S(1)}, bf16[512,1536]{1,0:T(8,128)(2,1)}, u32[]{:S(2)}) copy-start(bf16[512,1536]{1,0:T(8,128)(2,1)} %param.12) | copy-start | bytes 4718596
  1.6 19.2 %collective-permute-start = (bf16[4,16,512]{2,1,0:T(8,128)(2,1)S(1)}, bf16[4,16,512]{2,1,0:T(8,128)(2,1)S(1)}, u32[]{:S(2)}, u32[]{:S(2)}) collective-permute-start(bf16[4,16,512]{2,1,0:T(8,128)(2,1)S(1)} %get-tuple-element.12), channel_id=1, source_target_pairs={{0,8},{8,16},{16,24},{1,9},{9,17},{17,25},{2,10},{10,18},{18,26},{... | collective-permute-start | bytes 196616 | tf_op jit(solution)/shard_map/ppermute | solution.py:23
  4.9 17.0 %collective-permute-start.1 = (bf16[4,16,512]{2,1,0:T(8,128)(2,1)S(1)}, bf16[4,16,512]{2,1,0:T(8,128)(2,1)S(1)}, u32[]{:S(2)}, u32[]{:S(2)}) collective-permute-start(bf16[4,16,512]{2,1,0:T(8,128)(2,1)S(1)} %get-tuple-element.11), channel_id=1, source_target_pairs={{8,0},{16,8},{24,16},{9,1},{17,9},{25,17},{10,2},{18,10},{26,18},{... | collective-permute-start | bytes 196616 | tf_op jit(solution)/shard_map/ppermute | solution.py:26
  22.0 8.4 %collective-permute-start.2 = (bf16[24,4,512]{2,1,0:T(4,128)(2,1)S(1)}, bf16[24,4,512]{2,1,0:T(4,128)(2,1)S(1)}, u32[]{:S(2)}, u32[]{:S(2)}) collective-permute-start(bf16[24,4,512]{2,1,0:T(4,128)(2,1)S(1)} %get-tuple-element.9), channel_id=1, source_target_pairs={{0,1},{1,2},{2,3},{3,4},{4,5},{5,6},{6,7},{8,9},{9,10},{10,11},{11... | collective-permute-start | bytes 294920 | tf_op jit(solution)/shard_map/ppermute | solution.py:23
  28.2 6.8 %collective-permute-start.3 = (bf16[24,4,512]{2,1,0:T(4,128)(2,1)S(1)}, bf16[24,4,512]{2,1,0:T(4,128)(2,1)S(1)}, u32[]{:S(2)}, u32[]{:S(2)}) collective-permute-start(bf16[24,4,512]{2,1,0:T(4,128)(2,1)S(1)} %get-tuple-element.10), channel_id=1, source_target_pairs={{1,0},{2,1},{3,2},{4,3},{5,4},{6,5},{7,6},{9,8},{10,9},{11,10},{12... | collective-permute-start | bytes 294920 | tf_op jit(solution)/shard_map/ppermute | solution.py:26
  64.4 2.6 %copy-start.3 = (bf16[9,64,1,16,32]{1,4,3,0,2:T(8,128)(2,1)S(1)}, bf16[9,64,1,16,32]{1,4,3,0,2:T(8,128)(2,1)}, u32[]{:S(2)}) copy-start(bf16[9,64,1,16,32]{1,4,3,0,2:T(8,128)(2,1)} %copy.29) | copy-start | bytes 1769476
  70.7 4.0 %copy-start.5 = (bf16[512,512]{1,0:T(8,128)(2,1)S(1)}, bf16[512,512]{1,0:T(8,128)(2,1)}, u32[]{:S(2)}) copy-start(bf16[512,512]{1,0:T(8,128)(2,1)} %param.13) | copy-start | bytes 1572868
  70.7 4.6 %copy-start.2 = (bf16[16,16,512]{2,1,0:T(8,128)(2,1)S(1)}, bf16[16,16,512]{2,1,0:T(8,128)(2,1)}, u32[]{:S(2)}) copy-start(bf16[16,16,512]{2,1,0:T(8,128)(2,1)} %param.8) | copy-start | bytes 786436
  118.1 2.2 %copy-start.4 = (bf16[1,512,512]{2,1,0:T(8,128)(2,1)S(1)}, bf16[1,512,512]{2,1,0:T(8,128)(2,1)}, u32[]{:S(2)}) copy-start(bf16[1,512,512]{2,1,0:T(8,128)(2,1)} %param.14) | copy-start | bytes 1572868
  121.3 2.3 %copy-start.6 = (bf16[1,512,512]{2,1,0:T(8,128)(2,1)S(1)}, bf16[1,512,512]{2,1,0:T(8,128)(2,1)}, u32[]{:S(2)}) copy-start(bf16[1,512,512]{2,1,0:T(8,128)(2,1)} %param.15) | copy-start | bytes 1572868
  132.5 53.2 %copy-start.1 = (bf16[256,512]{1,0:T(8,128)(2,1)S(1)}, bf16[256,512]{1,0:T(8,128)(2,1)}, u32[]{:S(2)}) copy-start(bf16[256,512]{1,0:T(8,128)(2,1)} %fusion.23.refs_1_) | copy-start | bytes 786436

commit v2 on v1

--- a/solution.py
+++ b/solution.py
@@ -2,6 +2,7 @@
 
 import jax
 import jax.numpy as jnp
+import numpy as np
 from jax import lax
 from jax.experimental import pallas as pl
 from jax.experimental.pallas import tpu as pltpu
@@ -46,36 +47,48 @@
     return centred * lax.rsqrt(spread + 1e-05)
 
 
-def window_attend(qkv, in_grid):
-    ext_rows, ext_cols, triple = qkv.shape
-    feature = triple // 3
+def window_order(tile_rows, tile_cols):
+    wins = (tile_cols + 2 * margin_cells) // window_side
+    rows = (np.arange(tile_rows) + margin_cells) // window_side
+    cols = (np.arange(tile_cols) + margin_cells) // window_side
+    window = (rows[:, None] * wins + cols[None, :]).reshape(-1)
+    order = np.argsort(window, kind="stable")
+    counts = np.bincount(window)
+    return order, tuple((int(c.sum()), int(n)) for c, n in ((counts[:i], counts[i]) for i in range(len(counts))))
+
+
+def attend_window(number, first, amount, queries, keys_values, absent, context):
+    feature = queries.shape[1]
     head_size = feature // HEADS
-    win_rows = ext_rows // window_side
-    win_cols = ext_cols // window_side
     cells = window_side * window_side
-    blocks = qkv.reshape(win_rows, window_side, win_cols, window_side, triple).transpose(
-        0, 2, 1, 3, 4
-    )
-    blocks = blocks.reshape(win_rows * win_cols, cells, 3, HEADS, head_size)
-    present = (
-        in_grid.reshape(win_rows, window_side, win_cols, window_side)
-        .transpose(0, 2, 1, 3)
-        .reshape(win_rows * win_cols, cells)
-    )
-    scores = jnp.einsum(
-        "wqhd,wkhd->whqk", blocks[:, :, 0], blocks[:, :, 1], preferred_element_type=jnp.float32
-    ) / math.sqrt(head_size)
-    scores = jnp.where(present[:, None, None, :], scores, jnp.float32(-1e30))
-    peak_score = jnp.max(scores, axis=-1, keepdims=True)
-    weights = jnp.exp(scores - peak_score)
-    probabilities = (weights / jnp.sum(weights, axis=-1, keepdims=True)).astype(jnp.bfloat16)
-    context = jnp.einsum(
-        "whqk,wkhd->wqhd", probabilities, blocks[:, :, 2], preferred_element_type=jnp.float32
-    ).astype(jnp.bfloat16)
-    context = context.reshape(win_rows, win_cols, window_side, window_side, feature).transpose(
-        0, 2, 1, 3, 4
-    )
-    return context.reshape(ext_rows, ext_cols, feature)
+    group = 128 // head_size
+    mine = pl.ds(first, amount)
+    theirs = pl.ds(number * cells, cells)
+    lane = lax.broadcasted_iota(jnp.int32, (amount, 128), 1)
+    keep = [
+        ((lane >= h * head_size) & (lane < (h + 1) * head_size)).astype(jnp.float32)
+        for h in range(group)
+    ]
+    for start in range(0, feature, 128):
+        query = queries[mine, pl.ds(start, 128)]
+        stacked = jnp.concatenate([query * k.astype(jnp.bfloat16) for k in keep], axis=0)
+        scores = lax.dot_general(
+            stacked,
+            keys_values[theirs, pl.ds(start, 128)],
+            (((1,), (1,)), ((), ())),
+            preferred_element_type=jnp.float32,
+        ) / math.sqrt(head_size)
+        scores = scores + absent[pl.ds(number, 1), :]
+        weights = jnp.exp(scores - jnp.max(scores, axis=-1, keepdims=True))
+        total = jnp.sum(weights, axis=-1, keepdims=True)
+        probabilities = (weights * (1.0 / total)).astype(jnp.bfloat16)
+        mixed = jnp.dot(
+            probabilities,
+            keys_values[theirs, pl.ds(feature + start, 128)],
+            preferred_element_type=jnp.float32,
+        )
+        picked = sum(k * mixed[h * amount : (h + 1) * amount] for h, k in enumerate(keep))
+        context[mine, pl.ds(start, 128)] = picked.astype(jnp.bfloat16)
 
 
 def enter(ring, ranks):
@@ -125,10 +138,24 @@
 
 
 def spread_kernel(
-    count, ring, ranks, cap, values, placers, out, held, slots, z_send, z_recv, a_send, a_recv
+    windows, ring, ranks, cap,
+    upstream, tokens, extended, absent, marks, order, back_order, w_qkv, w_proj,
+    out, placers, mixed,
+    held, slots, known, queries, keys_values, context,
+    z_send, z_recv, m_send, m_recv, a_send, a_recv,
 ):
     row = lax.axis_index("rep")
+    feature = tokens.shape[1]
     enter(ring, ranks)
+
+    def pass_marks(origin, source, side):
+        pltpu.make_async_remote_copy(
+            src_ref=source,
+            dst_ref=known.at[origin],
+            send_sem=m_send.at[origin, (side + 1) // 2],
+            recv_sem=m_recv.at[origin],
+            device_id={"rep": row + side},
+        ).start()
 
     def pass_on(t, origin, source, side):
         pltpu.make_async_remote_copy(
@@ -139,49 +166,92 @@
             device_id={"rep": row + side},
         ).start()
 
-    def dispatch(t, origin, tokens):
+    def make_placer(origin, ids):
+        slot_ids = lax.broadcasted_iota(jnp.int32, placers.shape[1:], 0)
+        placers[origin] = (slot_ids == ids).astype(jnp.float32).astype(jnp.bfloat16)
+
+    def dispatch(t, origin, values):
         slots[t, origin] = jnp.dot(
-            placers[origin], tokens, preferred_element_type=jnp.float32
+            placers[origin], values, preferred_element_type=jnp.float32
         ).astype(jnp.bfloat16)
         swap_start(
             ring, cap, slots.at[t, origin], out.at[t, origin], a_send.at[t, origin], a_recv.at[t, origin]
         )
 
-    for t in range(count):
-
+    def own(t, source):
         @pl.when(row < ranks - 1)
         def _():
-            pass_on(t, row, values[t], 1)
+            if t == 0:
+                pass_marks(row, marks, 1)
+            pass_on(t, row, source, 1)
 
         @pl.when(row > 0)
         def _():
-            pass_on(t, row, values[t], -1)
-
-    for t in range(count):
-        dispatch(t, row, values[t][...])
-
-    def step(k, carry):
-        for t in range(count):
+            if t == 0:
+                pass_marks(row, marks, -1)
+            pass_on(t, row, source, -1)
+
+        if t == 0:
+            make_placer(row, marks[0:1, :])
+        dispatch(t, row, source[...])
+
+    def steps(t, begin, end):
+        def step(k, carry):
             for side in (1, -1):
                 origin = row - side * k
 
                 @pl.when((origin >= 0) & (origin < ranks))
                 def _():
+                    onward = row + side
+                    inner = (onward >= 0) & (onward < ranks)
+                    if t == 0:
+                        await_bytes(known.at[origin], m_recv.at[origin])
+
+                        @pl.when(inner)
+                        def _():
+                            pass_marks(origin, known.at[origin], side)
+
                     await_bytes(held.at[t, origin], z_recv.at[t, origin])
-                    onward = row + side
-
-                    @pl.when((onward >= 0) & (onward < ranks))
+
+                    @pl.when(inner)
                     def _():
                         pass_on(t, origin, held.at[t, origin], side)
 
+                    if t == 0:
+                        make_placer(origin, known[origin, 0:1, :])
                     dispatch(t, origin, held[t, origin])
 
-        return carry
-
-    lax.fori_loop(1, ranks, step, 0)
+            return carry
+
+        lax.fori_loop(begin, end, step, 0)
+
+    own(0, upstream)
+    keys_values[...] = jnp.dot(
+        extended[...], w_qkv[:, feature:], preferred_element_type=jnp.float32
+    ).astype(jnp.bfloat16)
+    grouped = jnp.dot(order[...], tokens[...], preferred_element_type=jnp.float32)
+    queries[...] = jnp.dot(
+        grouped.astype(jnp.bfloat16), w_qkv[:, :feature], preferred_element_type=jnp.float32
+    ).astype(jnp.bfloat16)
+    rounds = 3
+    for part in range(rounds):
+        low, high = (len(windows) * p // rounds for p in (part, part + 1))
+        for number in range(low, high):
+            attend_window(number, *windows[number], queries, keys_values, absent, context)
+        begin, end = (1 + (ranks - 1) * p // rounds for p in (part, part + 1))
+        if part < rounds - 1 and begin < end:
+            steps(0, begin, end)
+    ungrouped = jnp.dot(back_order[...], context[...], preferred_element_type=jnp.float32)
+    attended = jnp.dot(
+        ungrouped.astype(jnp.bfloat16), w_proj[...], preferred_element_type=jnp.float32
+    )
+    mixed[...] = (tokens[...].astype(jnp.float32) + layer_norm(attended)).astype(jnp.bfloat16)
+    own(1, mixed)
+    steps(0, 1 + (ranks - 1) * (rounds - 1) // rounds, ranks)
+    steps(1, 1, ranks)
 
     def finish(origin, carry):
-        for t in range(count):
+        for t in range(2):
             await_bytes(out.at[t, origin], a_recv.at[t, origin])
             sent = slots.at[t, origin, pl.ds(0, (ring - 1) * cap)]
             await_bytes(sent, a_send.at[t, origin])
@@ -189,10 +259,14 @@
             @pl.when((origin <= row) & (row < ranks - 1))
             def _():
                 await_bytes(held.at[t, origin], z_send.at[t, origin, 1])
+                if t == 0:
+                    await_bytes(known.at[origin], m_send.at[origin, 1])
 
             @pl.when((origin >= row) & (row > 0))
             def _():
                 await_bytes(held.at[t, origin], z_send.at[t, origin, 0])
+                if t == 0:
+                    await_bytes(known.at[origin], m_send.at[origin, 0])
 
         return carry
 
@@ -228,7 +302,12 @@
 
     def placed(t, target):
         await_bytes(back.at[t, target], a_recv.at[t, target])
-        return jnp.dot(placers[target], back[t, target], preferred_element_type=jnp.float32)
+        return lax.dot_general(
+            placers[target],
+            back[t, target],
+            (((0,), (0,)), ((), ())),
+            preferred_element_type=jnp.float32,
+        )
 
     def step(index, carry):
         k = ranks - index
@@ -296,38 +375,48 @@
     return [pl.BlockSpec(memory_space=pltpu.VMEM)] * amount
 
 
-def spread(values, placers, ring, ranks, cap):
-    count = len(values)
-    tok, feature = values[0].shape
+def spread(operands, windows, ring, ranks, cap):
+    tok, feature = operands[1].shape
+    ext_count = operands[2].shape[0]
+    rows = ring * cap
 
     def body(*refs):
-        spread_kernel(count, ring, ranks, cap, refs[:count], *refs[count:])
-
-    rows = ring * cap
+        spread_kernel(windows, ring, ranks, cap, *refs)
+
     return pl.pallas_call(
         body,
         name="spread",
-        out_shape=jax.ShapeDtypeStruct((count, ranks, rows, feature), jnp.bfloat16),
-        in_specs=in_vmem(count + 1),
-        out_specs=pl.BlockSpec(memory_space=pltpu.VMEM),
+        out_shape=(
+            jax.ShapeDtypeStruct((2, ranks, rows, feature), jnp.bfloat16),
+            jax.ShapeDtypeStruct((ranks, rows, tok), jnp.bfloat16),
+            jax.ShapeDtypeStruct((tok, feature), jnp.bfloat16),
+        ),
+        in_specs=in_vmem(len(operands)),
+        out_specs=tuple(in_vmem(3)),
         scratch_shapes=[
-            pltpu.VMEM((count, ranks, tok, feature), jnp.bfloat16),
-            pltpu.VMEM((count, ranks, rows, feature), jnp.bfloat16),
-            pltpu.SemaphoreType.DMA((count, ranks, 2)),
-            pltpu.SemaphoreType.DMA((count, ranks)),
-            pltpu.SemaphoreType.DMA((count, ranks)),
-            pltpu.SemaphoreType.DMA((count, ranks)),
+            pltpu.VMEM((2, ranks, tok, feature), jnp.bfloat16),
+            pltpu.VMEM((2, ranks, rows, feature), jnp.bfloat16),
+            pltpu.VMEM((ranks, 8, tok), jnp.int32),
+            pltpu.VMEM((tok, feature), jnp.bfloat16),
+            pltpu.VMEM((ext_count, 2 * feature), jnp.bfloat16),
+            pltpu.VMEM((tok, feature), jnp.bfloat16),
+            pltpu.SemaphoreType.DMA((2, ranks, 2)),
+            pltpu.SemaphoreType.DMA((2, ranks)),
+            pltpu.SemaphoreType.DMA((ranks, 2)),
+            pltpu.SemaphoreType.DMA((ranks,)),
+            pltpu.SemaphoreType.DMA((2, ranks)),
+            pltpu.SemaphoreType.DMA((2, ranks)),
         ],
         compiler_params=pltpu.CompilerParams(
             collective_id=0, has_side_effects=True, vmem_limit_bytes=60 << 20
         ),
-    )(*values, placers)
+    )(*operands)
 
 
 def collect(parts, placers, ring, ranks, cap):
     count = len(parts)
     rows, feature = parts[0].shape[1:]
-    tok = placers.shape[1]
+    tok = placers.shape[2]
 
     def body(*refs):
         collect_kernel(count, ring, ranks, cap, refs[:count], *refs[count:])
@@ -358,10 +447,12 @@
     ext_rows = tile_rows + 2 * margin_cells
     ext_cols = tile_cols + 2 * margin_cells
     extended = padded(tokens, (("rep", 0), ("exp", 1)), 4)
-    qkv = jnp.dot(extended.reshape(-1, feature), w_qkv, preferred_element_type=jnp.float32).astype(
-        jnp.bfloat16
-    )
-    qkv = qkv.reshape(ext_rows, ext_cols, 3 * feature)
+    win_rows, win_cols = ext_rows // window_side, ext_cols // window_side
+
+    def by_window(cells):
+        split = cells.reshape(win_rows, window_side, win_cols, window_side, -1)
+        return split.transpose(0, 2, 1, 3, 4).reshape(win_rows * win_cols, window_side**2, -1)
+
     row_ids = (
         lax.axis_index("rep") * tile_rows - margin_cells + jnp.arange(ext_rows, dtype=jnp.int32)
     )
@@ -371,12 +462,12 @@
     row_inside = (row_ids >= 0) & (row_ids < tile_rows * lax.axis_size("rep"))
     col_inside = (col_ids >= 0) & (col_ids < tile_cols * lax.axis_size("exp"))
     in_grid = row_inside[:, None] & col_inside[None, :]
-    context = window_attend(qkv, in_grid)[
-        margin_cells : tile_rows + margin_cells, margin_cells : tile_cols + margin_cells
-    ].reshape(tok_count, feature)
-    attended = jnp.dot(context, w_proj, preferred_element_type=jnp.float32)
+    absent = jnp.where(by_window(in_grid)[..., 0], 0.0, -1e30).astype(jnp.float32)
     flat_tokens = tokens.reshape(tok_count, feature)
-    mixed = (flat_tokens.astype(jnp.float32) + layer_norm(attended)).astype(jnp.bfloat16)
+    order, windows = window_order(tile_rows, tile_cols)
+    grouping = np.zeros((tok_count, tok_count), np.float32)
+    grouping[np.arange(tok_count), order] = 1.0
+    grouping = jnp.asarray(grouping, jnp.bfloat16)
     experts = lax.axis_size("exp")
     ranks = lax.axis_size("rep")
     capacity = max(2, 3 * tok_count // (2 * experts))
@@ -385,15 +476,23 @@
     chosen = route.reshape(tok_count)
     matches = (chosen[:, None] == jnp.arange(experts, dtype=jnp.int32)[None, :]).astype(jnp.int32)
     position = jnp.sum(matches * (jnp.cumsum(matches, axis=0) - 1), axis=1)
-    targets = lax.all_gather(chosen * capacity + position, "rep")
-    slot_ids = jnp.arange(slot_count, dtype=jnp.int32)
-    to_slots = (slot_ids[None, :, None] == targets[:, None, :]).astype(jnp.bfloat16)
-    from_slots = (targets[:, :, None] == slot_ids[None, None, :]).astype(jnp.bfloat16)
+    marks = jnp.broadcast_to((chosen * capacity + position)[None, :], (8, tok_count))
     gate_rows = gate.reshape(tok_count)
     upstream = (
         gate_rows[:, None] * cotangent.reshape(tok_count, feature).astype(jnp.float32)
     ).astype(jnp.bfloat16)
-    gathered = spread((upstream, mixed), to_slots, experts, ranks, capacity)
+    operands = (
+        upstream,
+        flat_tokens,
+        by_window(extended).reshape(-1, feature),
+        absent,
+        marks,
+        grouping,
+        grouping.T,
+        w_qkv,
+        w_proj,
+    )
+    gathered, placers, mixed = spread(operands, windows, experts, ranks, capacity)
     slot_grads = gathered[0].reshape(-1, feature)
     slot_rows = gathered[1].reshape(-1, feature)
     up_mat = w_up[0]
@@ -410,7 +509,7 @@
     input_slots = jnp.dot(pre_grad, up_mat, preferred_element_type=jnp.float32).astype(jnp.bfloat16)
     shape = (ranks, slot_count, feature)
     returned = collect(
-        (expert_out.reshape(shape), input_slots.reshape(shape)), from_slots, experts, ranks, capacity
+        (expert_out.reshape(shape), input_slots.reshape(shape)), placers, experts, ranks, capacity
     )
     layer_out = (mixed.astype(jnp.float32) + gate_rows[:, None] * returned[0]).astype(jnp.bfloat16)
     input_grad = returned[1].astype(jnp.bfloat16)

time: 190 us -> 142 us (0.75)
  local copies, waits for them, and re-layouts: 39.8 us -> 9.09 us
  blocking collectives: 6.21 us -> 0 us
  other arithmetic: 12.6 us -> 6.79 us
  matrix products: 16.6 us -> 12.3 us
  starting transfers between devices: 13.5 us -> 11.4 us
  Pallas kernels: 95.1 us -> 97.1 us
    unnamed x20 -> x8, local copies, waits for them, and re-layouts: 13.2 us -> 1 us
    reshape x2 -> x1, local copies, waits for them, and re-layouts: 10.4 us -> 0.87 us  [by_window(): split = cells.reshape(win_rows, window_side, win_cols, window_side, -1)]
    slice x3 -> x1, local copies, waits for them, and re-layouts: 7.17 us -> 0.21 us  [the longest x1 6.86 us: window_attend(): blocks[:, :, 2]]
    all_gather x1 -> x0, blocking collectives: 6.21 us -> none  [per_device(): targets = lax.all_gather(chosen * capacity + position, 'rep')]
    dot_general x4 -> x0, matrix products: 4.33 us -> none  [the longest x1 2.09 us: window_attend(): jnp.einsum('wqhd,wkhd->whqk', blocks[:, :, 0], blocks[:, :, 1], preferred...]
    convert_element_type x3 -> x0, other arithmetic: 3.07 us -> none  [the longest x1 1.13 us: per_device(): (slot_ids[None, :, None] == targets[:, None, :]).astype(jnp.bfloat16)]
    convert_element_type x1 -> x0, local copies, waits for them, and re-layouts: 2.95 us -> none  [window_attend(): context = jnp.einsum('whqk,wkhd->wqhd', probabilities, blocks[:, :, 2], p...]
    pallas_call x1, Pallas kernels: 41.9 us -> 44.6 us  [spread(): pl.pallas_call(body, name='spread', out_shape=(jax.ShapeDtypeStruct((2, r...]
where the time goes in v2:
time: 142 us; the launch traced here: 141 us
  Pallas kernels  97.1 us (68%)
  matrix products  12.3 us (9%)
  starting transfers between devices  11.4 us (8%)
  local copies, waits for them, and re-layouts  9.09 us (6%)
  other arithmetic  6.79 us (5%)
  waiting for transfers between devices  3.54 us (2%)
    pallas_call x1, Pallas kernels, collect(): pl.pallas_call(body, name='collect', out_shape=jax.ShapeDtypeStruct((coun...  52.5 us
    pallas_call x1, Pallas kernels, spread(): pl.pallas_call(body, name='spread', out_shape=(jax.ShapeDtypeStruct((2, r...  44.6 us
    ppermute x2, starting transfers between devices, padded(): lax.ppermute(lax.slice_in_dim(block, block.shape[dim] - width, None, axis...  7.44 us
    ppermute x2, starting transfers between devices, padded(): lax.ppermute(lax.slice_in_dim(block, 0, width, axis=dim), axis, backward)  4 us
    ppermute x2, waiting for transfers between devices, padded(): lax.ppermute(lax.slice_in_dim(block, 0, width, axis=dim), axis, backward)  3.54 us
  transfers between devices with their start and end apart: 4, of which 1 were waited for; matrix products, arithmetic and copies ran while one was open for 5% of the time, Pallas kernels for 0%

profile of v2, /device:TPU:11, one launch (start us, length us, event | category | flops | bytes accessed | tf_op | source)
XLA Modules:
  0.0 141.0 jit_solution(14513694470177304254)
XLA Ops:
  0.6 0.9 fusion.28
  1.6 2.1 %collective-permute-start.1 = (bf16[4,16,512]{2,1,0:T(8,128)(2,1)S(1)}, bf16[4,16,512]{2,1,0:T(8,128)(2,1)S(1)}, u32[]{:S(2)}, u32[]{:S(2)}) collective-permute-start(bf16[4,16,512]{2,1,0:T(8,128)(2,1)S(1)} %get-tuple-element.14), channel_id=1, source_target_pairs={{8,0},{16,8},{24,16},{9,1},{17,9},{25,17},{10,2},{18,10},{26,18},{... | collective-permute-start | bytes 196616 | tf_op jit(solution)/shard_map/ppermute | solution.py:27
  3.7 3.2 %collective-permute-start = (bf16[4,16,512]{2,1,0:T(8,128)(2,1)S(1)}, bf16[4,16,512]{2,1,0:T(8,128)(2,1)S(1)}, u32[]{:S(2)}, u32[]{:S(2)}) collective-permute-start(bf16[4,16,512]{2,1,0:T(8,128)(2,1)S(1)} %get-tuple-element.15), channel_id=1, source_target_pairs={{0,8},{8,16},{16,24},{1,9},{9,17},{17,25},{2,10},{10,18},{18,26},{... | collective-permute-start | bytes 196616 | tf_op jit(solution)/shard_map/ppermute | solution.py:24
  6.9 0.8 mul.91
  7.7 0.7 fusion.17
  9.3 1.8 %fusion.8.refs_0_ = bf16[256,512]{1,0:T(8,128)(2,1)} fusion(bf16[16,16,512]{2,1,0:T(8,128)(2,1)} %param.12, f32[256]{0:T(256)S(1)} %mul.91), kind=kLoop, calls=%fused_computation.19 | loop fusion | flops 393216 | bytes 525312 | tf_op jit(solution)/shard_map/convert_element_type | solution.py:483
  11.0 0.8 fusion.16
  11.8 1.0 constant_dynamic-update-slice_fusion.1
  12.9 4.2 %collective-permute-start.2 = (bf16[24,4,512]{2,1,0:T(4,128)(2,1)S(1)}, bf16[24,4,512]{2,1,0:T(4,128)(2,1)S(1)}, u32[]{:S(2)}, u32[]{:S(2)}) collective-permute-start(bf16[24,4,512]{2,1,0:T(4,128)(2,1)S(1)} %get-tuple-element.12), channel_id=1, source_target_pairs={{0,1},{1,2},{2,3},{3,4},{4,5},{5,6},{6,7},{8,9},{9,10},{10,11},{11... | collective-permute-start | bytes 294920 | tf_op jit(solution)/shard_map/ppermute | solution.py:24
  17.2 1.9 %collective-permute-start.3 = (bf16[24,4,512]{2,1,0:T(4,128)(2,1)S(1)}, bf16[24,4,512]{2,1,0:T(4,128)(2,1)S(1)}, u32[]{:S(2)}, u32[]{:S(2)}) collective-permute-start(bf16[24,4,512]{2,1,0:T(4,128)(2,1)S(1)} %get-tuple-element.13), channel_id=1, source_target_pairs={{1,0},{2,1},{3,2},{4,3},{5,4},{6,5},{7,6},{9,8},{10,9},{11,10},{12... | collective-permute-start | bytes 294920 | tf_op jit(solution)/shard_map/ppermute | solution.py:27
  19.1 0.7 multiply_add_fusion.2
  20.5 3.5 %collective-permute-done.3 = bf16[24,4,512]{2,1,0:T(4,128)(2,1)S(1)} collective-permute-done((bf16[24,4,512]{2,1,0:T(4,128)(2,1)S(1)}, bf16[24,4,512]{2,1,0:T(4,128)(2,1)S(1)}, u32[]{:S(2)}, u32[]{:S(2)}) %collective-permute-start.3) | collective-permute-done | bytes 98336 | tf_op jit(solution)/shard_map/ppermute | solution.py:27
  24.3 0.9 copy.14
  25.8 44.6 %spread.1 = (bf16[2,4,384,512]{3,2,1,0:T(8,128)(2,1)}, bf16[4,384,256]{2,1,0:T(8,128)(2,1)}, bf16[256,512]{1,0:T(8,128)(2,1)}) custom-call(bf16[256,512]{1,0:T(8,128)(2,1)} %fusion.8.refs_0_, bf16[256,512]{1,0:T(8,128)(2,1)} %bitcast.58, bf16[576,512]{1,0:T(8,128)(2,1)} %bitcast.57, f32[9,64]{1,0:T(8,128)} %select_n.10.refs_3_, ...), custom_call_target="tpu_custom_call" | custom-call | tf_op jit(solution)/shard_map/spread/pallas_call | solution.py:386
  70.4 2.1 %fusion.26 = (bf16[1,4,384,512]{3,2,1,0:T(8,128)(2,1)S(1)}, bf16[1,4,384,512]{3,2,1,0:T(8,128)(2,1)S(1)}) fusion(bf16[2,4,384,512]{3,2,1,0:T(8,128)(2,1)} %get-tuple-element.8), kind=kLoop, calls=%fused_computation.48 | loop fusion | bytes 6291456 | tf_op jit(solution)/shard_map/slice | solution.py:496
  72.6 1.0 fusion.14
  73.6 2.3 %fusion.6 = f32[1,512,512]{2,1,0:T(8,128)} fusion(bf16[1536,512]{1,0:T(8,128)(2,1)S(1)} %bitcast.61, f32[1536,512]{1,0:T(8,128)S(1)} %fusion.14), kind=kOutput, calls=%fused_computation.13 | convolution fusion | flops 812646400 | bytes 5767168 | tf_op jit(solution)/shard_map/dot_general | solution.py:520
  76.0 2.4 %fusion.5 = bf16[1536,512]{1,0:T(8,128)(2,1)S(1)} fusion(f32[1536,512]{1,0:T(8,128)S(1)} %fusion.14, bf16[1536,512]{1,0:T(8,128)(2,1)S(1)} %bitcast.62, bf16[1,512,512]{2,1,0:T(8,128)(2,1)S(1)} %copy-done), kind=kOutput, calls=%fused_computation.11 | convolution fusion | flops 820248576 | bytes 6815744 | tf_op jit(solution)/shard_map/dot_general | solution.py:505
  78.4 2.4 %convolution_convert_fusion.1 = bf16[1536,512]{1,0:T(8,128)(2,1)} fusion(bf16[1,512,512]{2,1,0:T(8,128)(2,1)S(1)} %copy-done, f32[1536,512]{1,0:T(8,128)S(1)} %fusion.14), kind=kOutput, calls=%fused_computation.10 | convolution fusion | flops 813170688 | bytes 5242880 | tf_op jit(solution)/shard_map/dot_general | solution.py:504
  80.8 2.0 %fusion.7 = f32[1,512,512]{2,1,0:T(8,128)} fusion(bf16[1536,512]{1,0:T(8,128)(2,1)S(1)} %fusion.5, bf16[1536,512]{1,0:T(8,128)(2,1)S(1)} %bitcast.55), kind=kOutput, calls=%fused_computation.15 | convolution fusion | flops 805568512 | bytes 4194304 | tf_op jit(solution)/shard_map/dot_general | solution.py:517
  82.7 2.1 %convolution_convert_fusion = bf16[1536,512]{1,0:T(8,128)(2,1)} fusion(bf16[1536,512]{1,0:T(8,128)(2,1)S(1)} %fusion.5, bf16[1,512,512]{2,1,0:T(8,128)(2,1)S(1)} %copy-done.1), kind=kOutput, calls=%fused_computation.9 | convolution fusion | flops 806092800 | bytes 3670016 | tf_op jit(solution)/shard_map/dot_general | solution.py:509
  84.9 52.5 %collect.1 = f32[2,256,512]{2,1,0:T(8,128)} custom-call(bf16[4,384,512]{2,1,0:T(8,128)(2,1)} %bitcast.59, bf16[4,384,512]{2,1,0:T(8,128)(2,1)} %bitcast.60, bf16[4,384,256]{2,1,0:T(8,128)(2,1)} %get-tuple-element.9.refs_2_), custom_call_target="tpu_custom_call" | custom-call | tf_op jit(solution)/shard_map/collect/pallas_call | solution.py:424
  137.4 1.8 %slice.48 = bf16[1,256,512]{2,1,0:T(8,128)(2,1)} slice(f32[2,256,512]{2,1,0:T(8,128)} %collect.1), slice={[1:2], [0:256], [0:512]} | slice | bytes 524288 | tf_op jit(solution)/shard_map/slice | solution.py:515
  139.1 1.9 %fusion.10 = bf16[256,512]{1,0:T(8,128)(2,1)} fusion(f32[2,256,512]{2,1,0:T(8,128)} %collect.1, bf16[256,512]{1,0:T(8,128)(2,1)S(1)} %copy-done.2, f32[256]{0:T(256)S(1)} %mul.91), kind=kLoop, calls=%fused_computation.22 | loop fusion | flops 524288 | bytes 1049600 | tf_op jit(solution)/shard_map/convert_element_type | solution.py:514
  (21 shorter events, 2.6 us)
Async XLA Ops:
  0.6 75.3 %copy-start = (bf16[1,512,512]{2,1,0:T(8,128)(2,1)S(1)}, bf16[1,512,512]{2,1,0:T(8,128)(2,1)}, u32[]{:S(2)}) copy-start(bf16[1,512,512]{2,1,0:T(8,128)(2,1)} %param.16) | copy-start | bytes 1572868
  1.6 11.2 %collective-permute-start.1 = (bf16[4,16,512]{2,1,0:T(8,128)(2,1)S(1)}, bf16[4,16,512]{2,1,0:T(8,128)(2,1)S(1)}, u32[]{:S(2)}, u32[]{:S(2)}) collective-permute-start(bf16[4,16,512]{2,1,0:T(8,128)(2,1)S(1)} %get-tuple-element.14), channel_id=1, source_target_pairs={{8,0},{16,8},{24,16},{9,1},{17,9},{25,17},{10,2},{18,10},{26,18},{... | collective-permute-start | bytes 196616 | tf_op jit(solution)/shard_map/ppermute | solution.py:27
  3.7 8.1 %collective-permute-start = (bf16[4,16,512]{2,1,0:T(8,128)(2,1)S(1)}, bf16[4,16,512]{2,1,0:T(8,128)(2,1)S(1)}, u32[]{:S(2)}, u32[]{:S(2)}) collective-permute-start(bf16[4,16,512]{2,1,0:T(8,128)(2,1)S(1)} %get-tuple-element.15), channel_id=1, source_target_pairs={{0,8},{8,16},{16,24},{1,9},{9,17},{17,25},{2,10},{10,18},{18,26},{... | collective-permute-start | bytes 196616 | tf_op jit(solution)/shard_map/ppermute | solution.py:24
  12.9 7.5 %collective-permute-start.2 = (bf16[24,4,512]{2,1,0:T(4,128)(2,1)S(1)}, bf16[24,4,512]{2,1,0:T(4,128)(2,1)S(1)}, u32[]{:S(2)}, u32[]{:S(2)}) collective-permute-start(bf16[24,4,512]{2,1,0:T(4,128)(2,1)S(1)} %get-tuple-element.12), channel_id=1, source_target_pairs={{0,1},{1,2},{2,3},{3,4},{4,5},{5,6},{6,7},{8,9},{9,10},{10,11},{11... | collective-permute-start | bytes 294920 | tf_op jit(solution)/shard_map/ppermute | solution.py:24
  17.2 6.8 %collective-permute-start.3 = (bf16[24,4,512]{2,1,0:T(4,128)(2,1)S(1)}, bf16[24,4,512]{2,1,0:T(4,128)(2,1)S(1)}, u32[]{:S(2)}, u32[]{:S(2)}) collective-permute-start(bf16[24,4,512]{2,1,0:T(4,128)(2,1)S(1)} %get-tuple-element.13), channel_id=1, source_target_pairs={{1,0},{2,1},{3,2},{4,3},{5,4},{6,5},{7,6},{9,8},{10,9},{11,10},{12... | collective-permute-start | bytes 294920 | tf_op jit(solution)/shard_map/ppermute | solution.py:27
  70.4 2.2 %copy-start.1 = (bf16[1,512,512]{2,1,0:T(8,128)(2,1)S(1)}, bf16[1,512,512]{2,1,0:T(8,128)(2,1)}, u32[]{:S(2)}) copy-start(bf16[1,512,512]{2,1,0:T(8,128)(2,1)} %param.15) | copy-start | bytes 1572868
  84.9 54.3 %copy-start.2 = (bf16[256,512]{1,0:T(8,128)(2,1)S(1)}, bf16[256,512]{1,0:T(8,128)(2,1)}, u32[]{:S(2)}) copy-start(bf16[256,512]{1,0:T(8,128)(2,1)} %get-tuple-element.7) | copy-start | bytes 786436
